TPU v7x, 32 devices: a whole 2x2x4 slice. The times are simulated.
32 devices in a mesh: dev: 32 (over z, y, x, core).
Axes of the slice: x: 2, y: 2, z: 4, core: 2. Of those that a mesh axis runs over, the one named last changes fastest.
Arguments:
- occurrence: bfloat16 [2048, 128, 128], P('dev'), may hold values from -0.5 to 0.5
- block_owner: int32 [2048, 1], P('dev'), may hold values from 0 to 31; in each aligned block of 64 rows (0 to 63, 64 to 127, ...) at most 4 rows name the same one
- read_block: int32 [2048], P('dev'), may hold values from 0 to 15
- slot_order: int32 [32, 128], P('dev'), may hold values from 0 to 127, each once within a row
Outputs:
- margin: float32 [65536, 512], P('dev')
Inputs may be any that keep to these rules, and one draw needn't show every extreme that they name: `block_owner`: among the blocks of one device no owner is named more than 4 times, a bound that some block reaches. `slot_order`: each row names every number of 0 to 127 once.
All inputs are finite; a program needn't handle non-finite values.
Results may differ from a plain program's by a relative error of at most 0.0026.
Values may be sent and summed in bfloat16 or wider, within the bound.
A program may use at most 128 MiB of HBM per device.

v0:
```python
import functools
import jax
import jax.numpy as jnp
import numpy as np
from jax import lax
from jax.experimental import pallas as pl
from jax.experimental.pallas import tpu as pltpu
from jax.sharding import PartitionSpec as P

CAP = 4
RB_DEV = 16
CORES = 2
HALVES = 2
FAMILY = CORES * HALVES


def i32(x):
    return x.astype(jnp.int32)


def iota(*shape, axis):
    return lax.broadcasted_iota(jnp.int32, shape, axis)


def group_table(owners, order):
    devices, blocks = owners.shape
    slots = order.shape[1]
    per_pair = slots // devices
    earlier = iota(blocks, blocks, axis=1) < iota(blocks, blocks, axis=0)
    same = owners[:, :, None] == owners[:, None, :]
    rank = jnp.sum(i32(same & earlier[None]), axis=2)
    key = owners * per_pair + rank
    number = iota(devices, blocks, axis=0) * blocks + iota(devices, blocks, axis=1) + 1
    hit = key[:, :, None] == iota(1, 1, slots, axis=2)
    holder = jnp.sum(jnp.where(hit, number[:, :, None], 0), axis=1)
    holder = holder.reshape(devices, devices, per_pair).transpose(1, 0, 2).reshape(devices, slots)
    turned = order.reshape(devices, slots // CAP, CAP).transpose(2, 0, 1)
    hit = turned[:, :, :, None] == iota(1, 1, 1, slots, axis=3)
    table = jnp.sum(jnp.where(hit, holder[None, :, None, :], 0), axis=3)
    return table.reshape(CAP, devices * slots // CAP)


def fullest_lane(table, blocks):
    devices = lax.axis_size("dev")
    families = devices // FAMILY
    chips = devices // CORES
    source = jnp.where(table > 0, (table - 1) // blocks, -1)
    named = source[:, :, None] == iota(1, 1, devices, axis=2)
    held = jnp.sum(i32(named), axis=0)
    held_chip = jnp.sum(held.reshape(-1, chips, CORES), axis=2)
    demand = jnp.einsum(
        "gc,gd->cd",
        held_chip.astype(jnp.bfloat16),
        (held > 0).astype(jnp.bfloat16),
        preferred_element_type=jnp.float32,
    )
    c, d = iota(chips, devices, axis=0), iota(chips, devices, axis=1)
    return jnp.max(jnp.where(c % families != d // CORES % families, demand, 0.0))


def routes(table, blocks):
    devices = lax.axis_size("dev")
    families = devices // FAMILY
    half_devices = devices // HALVES
    many = FAMILY * blocks
    me = lax.axis_index("dev")
    half, family, core = me // half_devices, me // CORES % families, me % CORES
    x = jnp.arange(many, dtype=jnp.int32)
    x_half, x_core, x_block = x // (CORES * blocks), x // blocks % CORES, x % blocks
    ids = (((x_half * families + family) * CORES + x_core) * blocks + x_block + 1)[:, None]
    inside = (table[0][None] == ids) | (table[1][None] == ids)
    for j in range(2, CAP):
        inside = inside | (table[j][None] == ids)
    partners = jnp.stack(
        [jnp.sum(jnp.where(inside, table[j][None], 0), axis=1) for j in range(CAP)]
    )
    source = jnp.where(partners > 0, (partners - 1) // blocks, -1)
    target = iota(1, half_devices, axis=1) + half * half_devices
    named = source[:, :, None] == target[None]
    need = jnp.any(named, axis=0) & (target // CORES % families != family)
    row, column = iota(many, many, axis=0), iota(many, many, axis=1)
    same_chip = row // (CORES * blocks) == column // (CORES * blocks)
    before = ((column < row) & same_chip).astype(jnp.bfloat16)
    rank = i32(jnp.dot(before, need.astype(jnp.bfloat16), preferred_element_type=jnp.float32))
    rank = jnp.where(need, rank, -1).T
    local = (i32(x_half != half) * CORES + i32(x_core != core)) * blocks + x_block

    begin = half * CORES * blocks + core * blocks
    own = lax.dynamic_slice(partners, (0, begin), (CAP, blocks)).reshape(-1)
    total = devices * blocks
    match = own[:, None] == iota(1, total, axis=1) + 1
    wanted = jnp.any(match, axis=0).reshape(HALVES, families, CORES * blocks)
    wanted = wanted.transpose(1, 0, 2).reshape(families, many)
    arrived = i32(
        jnp.dot(wanted.astype(jnp.bfloat16), before.T, preferred_element_type=jnp.float32)
    )
    f = iota(families, many, axis=0)
    part = i32(iota(families, many, axis=1) // (CORES * blocks) != half)

    def send(begin, lane, far):
        spot = begin + iota(1, lane, 1, axis=1) * CORES + core
        chosen = jnp.where((x_half != half) == far, local % (CORES * blocks), 0)
        hit = (rank[:, None, :] == spot) & ((x_half != half) == far)
        return jnp.sum(jnp.where(hit, chosen[None, None, :], 0), axis=2).reshape(-1)

    def pick(begin, lane, local):
        empty = many + HALVES * half_devices * lane
        now = arrived - begin
        there = (part * half_devices + f * CORES + now % CORES) * lane + now // CORES + many
        there = jnp.where((now >= 0) & (now < lane * CORES), there, empty)
        place = jnp.where(f == family, empty if local is None else local[None, :], there)
        place = place.reshape(families, HALVES, CORES * blocks).transpose(1, 0, 2).reshape(1, total)
        found = jnp.sum(jnp.where(match, place, 0), axis=1)
        return jnp.where(own > 0, found, empty)

    return send, pick, local


def fill(near, held, sems):
    blocks = near[0].shape[0]
    copies = [
        pltpu.make_async_copy(ref, held.at[pl.ds(i * blocks, blocks)], sems.at[i])
        for i, ref in enumerate(near)
    ]
    for copy in copies:
        copy.start()
    return copies


def pack_kernel(send_ref, a_ref, b_ref, out_ref, held, sems):
    for copy in fill((a_ref, b_ref), held, sems):
        copy.wait()

    def step(i, _):
        out_ref[i] = held[send_ref[i]]
        return 0

    lax.fori_loop(0, out_ref.shape[0], step, 0, unroll=4)


def tile_kernel(pick_ref, read_ref, *refs):
    near, got, (out_ref, held, sems) = refs[:FAMILY], refs[FAMILY:-3], refs[-3:]
    blocks, rows = near[0].shape[:2]
    base, many = FAMILY * blocks, got[0].shape[0]
    copies = fill(near, held, sems)
    for i, ref in enumerate(got):
        into = held.at[pl.ds(base + i * many, many)]
        copies.append(pltpu.make_async_copy(ref, into, sems.at[FAMILY + i]))
        copies[-1].start()
    held[base + HALVES * many] = jnp.zeros(held.shape[1:], held.dtype)
    out_ref[...] = jnp.zeros_like(out_ref)
    for copy in copies:
        copy.wait()

    def step(b, _):
        others = jnp.concatenate([held[pick_ref[j * blocks + b]] for j in range(CAP)], axis=0)
        tile = lax.dot_general(
            held[b], others, (((1,), (1,)), ((), ())), preferred_element_type=jnp.float32
        )
        where = pl.ds(pl.multiple_of(read_ref[b] * rows, rows), rows)
        out_ref[where, :] += tile.astype(jnp.bfloat16).astype(jnp.float32)
        return 0

    lax.fori_loop(0, blocks, step, 0, unroll=2)


SMEM = pl.BlockSpec(memory_space=pltpu.SMEM)
HBM = pl.BlockSpec(memory_space=pl.ANY)
VMEM = pl.BlockSpec(memory_space=pltpu.VMEM)


def pack(send, near):
    blocks, rows, kmers = near[0].shape
    return pl.pallas_call(
        pack_kernel,
        out_shape=jax.ShapeDtypeStruct((send.shape[0], rows, kmers), near[0].dtype),
        in_specs=[SMEM] + [HBM] * CORES,
        out_specs=VMEM,
        scratch_shapes=[
            pltpu.VMEM((CORES * blocks, rows, kmers), near[0].dtype),
            pltpu.SemaphoreType.DMA((CORES,)),
        ],
        compiler_params=pltpu.CompilerParams(vmem_limit_bytes=60 << 20),
        name="pack",
    )(send, *near)


def tiles(pick, read_block, near, got):
    blocks, rows, kmers = near[0].shape
    total = FAMILY * blocks + HALVES * got[0].shape[0] + 1
    return pl.pallas_call(
        tile_kernel,
        out_shape=jax.ShapeDtypeStruct((RB_DEV * rows, CAP * rows), jnp.float32),
        in_specs=[SMEM, SMEM] + [HBM] * (FAMILY + HALVES),
        out_specs=VMEM,
        scratch_shapes=[
            pltpu.VMEM((total, rows, kmers), near[0].dtype),
            pltpu.SemaphoreType.DMA((FAMILY + HALVES,)),
        ],
        compiler_params=pltpu.CompilerParams(vmem_limit_bytes=60 << 20),
        name="tiles",
    )(pick, read_block, *near, *got)


def everyone_kernel(devices, group, row_ref, out_ref, send_sems, recv_sems):
    me = lax.axis_index("dev")
    first = me // group * group
    out_ref[me] = row_ref[...]

    def spread(src, dst, to, k):
        copy = pltpu.make_async_remote_copy(
            src_ref=src,
            dst_ref=dst,
            send_sem=send_sems.at[k],
            recv_sem=recv_sems.at[k],
            device_id=(to,),
            device_id_type=pl.DeviceIdType.MESH,
        )
        copy.start()
        return copy

    near = [
        spread(row_ref, out_ref.at[me], first + (me - first + k) % group, k)
        for k in range(1, group)
    ]
    for copy in near:
        copy.wait()
    rows = out_ref.at[pl.ds(first, group)]
    far = [
        spread(rows, rows, (me + k * group) % devices, group + k)
        for k in range(1, devices // group)
    ]
    for copy in far:
        copy.wait()


def gather_rows(row):
    devices = lax.axis_size("dev")
    group = 1 << devices.bit_length() // 2
    return pl.pallas_call(
        functools.partial(everyone_kernel, devices, group),
        out_shape=jax.ShapeDtypeStruct((devices,) + row.shape, row.dtype),
        in_specs=[VMEM],
        out_specs=VMEM,
        scratch_shapes=[pltpu.SemaphoreType.DMA((group + devices // group,))] * 2,
        compiler_params=pltpu.CompilerParams(has_side_effects=True),
        name="gather_rows",
    )(row)


def flipped(value, mask):
    bit = 1
    while bit <= mask:
        if mask & bit:
            value = value + bit - 2 * bit * (value // bit % 2)
        bit *= 2
    return value


def exchange_kernel(devices, lane, out_ref, got_ref, send_sems, recv_sems):
    me = lax.axis_index("dev")
    count = devices // HALVES
    spot = me % count

    def copy_of(k):
        to = flipped(spot, k)
        return pltpu.make_async_remote_copy(
            src_ref=out_ref.at[pl.ds(to * lane, lane)],
            dst_ref=got_ref.at[pl.ds(spot * lane, lane)],
            send_sem=send_sems.at[k],
            recv_sem=recv_sems.at[k],
            device_id=(me - spot + to,),
            device_id_type=pl.DeviceIdType.MESH,
        )

    chips = count // CORES
    steps = []
    for mask in range(chips - 1, chips // 2 - 1, -1):
        for core in range(CORES):
            masks = [m for m in (mask, chips - 1 - mask) if m]
            steps.append([copy_of(m * CORES + core) for m in masks])
    for i, step in enumerate(steps):
        if i >= 2:
            for copy in steps[i - 2]:
                copy.wait_send()
        for copy in step:
            copy.start()
    for step in steps[-2:]:
        for copy in step:
            copy.wait_send()
    for step in steps:
        for copy in step:
            copy.wait_recv()


def exchange(out, lane):
    devices = lax.axis_size("dev")
    count = devices // HALVES
    return pl.pallas_call(
        functools.partial(exchange_kernel, devices, lane),
        out_shape=jax.ShapeDtypeStruct(out.shape, out.dtype),
        in_specs=[HBM],
        out_specs=HBM,
        scratch_shapes=[pltpu.SemaphoreType.DMA((count,))] * 2,
        compiler_params=pltpu.CompilerParams(has_side_effects=True),
        cost_estimate=pl.CostEstimate(
            flops=0, bytes_accessed=32 * out.size * out.dtype.itemsize, transcendentals=0
        ),
        name="exchange",
    )(out)


def shards(occurrence, block_owner, read_block, slot_order):
    devices = lax.axis_size("dev")
    blocks = occurrence.shape[0]
    slots = slot_order.shape[1]
    lane = 2 * (2 * blocks // devices) + 1
    spill = 2 * blocks // devices
    swap = [(d, d ^ 1) for d in range(devices)]
    across = [(d, (d + devices // HALVES) % devices) for d in range(devices)]
    row = jnp.stack([jnp.pad(block_owner[:, 0], (0, slots - blocks)), slot_order[0]])
    everyone = gather_rows(row)
    everyone, mine = lax.optimization_barrier((everyone, occurrence))
    far = lax.ppermute(mine, "dev", across)
    sibling = lax.ppermute(mine, "dev", swap)
    table = group_table(everyone[:, 0, :blocks], everyone[:, 1])
    most = i32(fullest_lane(table, blocks))
    send, pick, local = routes(table, blocks)
    begin = CORES * lane
    got = exchange(pack(send(0, lane, False), (occurrence, sibling)), lane)
    far, got = lax.optimization_barrier((far, got))
    distant = (far, lax.ppermute(far, "dev", swap))
    near = (occurrence, sibling) + distant
    also = exchange(pack(send(0, lane, True), distant), lane)
    first = tiles(pick(0, lane, local), read_block, near, (got, also))

    def more(carry):
        begin, margin = carry
        got = exchange(pack(send(begin, spill, False), near[:CORES]), spill)
        also = exchange(pack(send(begin, spill, True), distant), spill)
        added = tiles(pick(begin, spill, None), read_block, near, (got, also))
        return begin + CORES * spill, margin + added

    return lax.while_loop(lambda carry: carry[0] < most, more, (jnp.int32(begin), first))[1]


def solution(mesh):
    placed = (P("dev", None, None), P("dev", None), P("dev"), P("dev", None))
    return jax.shard_map(
        shards, mesh=mesh, in_specs=placed, out_specs=P("dev", None), check_vma=False
    )
```

profile of v0, /device:TPU:0, one launch (start us, length us, event | category | flops | bytes accessed | tf_op | source)
XLA Modules:
  0.0 222.7 jit_solution(10431108965221943658)
XLA Ops:
  0.0 0.8 pad_bitcast_fusion
  0.8 1.2 pad_add_fusion.1.row_ref
  2.0 17.9 %gather_rows.1 = s32[32,2,128]{2,1,0:T(2,128)} custom-call(s32[2,128]{1,0:T(2,128)} %pad_add_fusion.1.row_ref), custom_call_target="tpu_custom_call" | custom-call | tf_op jit(solution)/shard_map/gather_rows/pallas_call | solution.py:240
  20.0 0.8 collective-permute-start.1
  20.8 0.8 slice.27
  21.6 0.8 slice.26
  22.4 0.9 convert_reduce_fusion
  23.3 0.1 add_add_fusion.1
  23.4 0.7 select_reduce_fusion.8
  24.1 0.1 copy.25
  24.2 0.1 copy.26
  24.3 0.1 copy.27
  24.3 0.1 copy.23
  24.4 0.1 copy.24
  24.5 2.9 %select_reduce_fusion.3 = s32[4,32,32]{2,1,0:T(8,128)S(1)} fusion(s32[32,128]{1,0:T(8,128)S(1)} %copy.27, s32[4,32,32]{2,1,0:T(8,128)S(1)} %copy.24), kind=kLoop, calls=%fused_computation.70 | loop fusion | flops 1568768 | bytes 49152 | tf_op jit(solution)/shard_map/reduce_sum | solution.py:39
  27.5 0.1 gt.47
  27.6 0.1 sub.110
  27.7 0.1 eq.278
  27.8 0.1 eq.288
  27.9 0.1 eq.285
  28.0 0.1 eq.282
  28.2 0.9 select_reduce_fusion.7
  29.1 0.1 compare_reduce_fusion.1
  29.2 0.3 fusion.37
  29.5 0.5 select_reduce_fusion.9
  29.9 0.1 copy.28
  30.0 0.7 reshape.488.send_ref
  30.7 5.1 %pack.4.out_ref = bf16[144,128,128]{2,1,0:T(8,128)(2,1)} custom-call(s32[144]{0:T(256)} %reshape.488.send_ref, bf16[64,128,128]{2,1,0:T(8,128)(2,1)S(1)} %copy-done, bf16[64,128,128]{2,1,0:T(8,128)(2,1)} %collective-permute-done.b_ref.refs_1_), custom_call_target="tpu_custom_call" | custom-call | tf_op jit(solution)/shard_map/pack/pallas_call | solution.py:174
  35.8 101.6 %exchange.4.refs_4_ = bf16[144,128,128]{2,1,0:T(8,128)(2,1)} custom-call(bf16[144,128,128]{2,1,0:T(8,128)(2,1)} %pack.4.out_ref), custom_call_target="tpu_custom_call" | custom-call | bytes 150994944 | tf_op jit(solution)/shard_map/exchange/pallas_call | solution.py:299
  137.4 0.5 collective-permute-start.2
  137.9 0.1 constant_dynamic-slice_fusion
  138.0 0.1 reshape.484
  138.1 0.1 copy.29
  138.1 0.7 reshape.489.send_ref
  138.8 0.1 convert_reduce_fusion.1
  138.8 0.1 reshape.490
  138.9 0.2 reduce_sum.161
  139.1 0.8 fusion.38
  140.7 0.4 compare_reduce_fusion
  141.1 0.3 convolution_convert_fusion.1
  141.3 0.1 fusion.55
  141.4 0.4 fusion.36
  141.8 0.6 compare_select_fusion.12.pick_ref
  142.4 0.0 collective-permute-done.2.b_ref.refs_3_
  142.4 5.6 %pack.5.out_ref = bf16[144,128,128]{2,1,0:T(8,128)(2,1)} custom-call(s32[144]{0:T(256)} %reshape.489.send_ref, bf16[64,128,128]{2,1,0:T(8,128)(2,1)} %collective-permute-done.1.a_ref.refs_2_, bf16[64,128,128]{2,1,0:T(8,128)(2,1)} %collective-permute-done.2.b_ref.refs_3_), custom_call_target="tpu_custom_call" | custom-call | tf_op jit(solution)/shard_map/pack/pallas_call | solution.py:174
  148.0 0.0 copy-start.1
  148.1 58.6 %exchange.5.refs_5_ = bf16[144,128,128]{2,1,0:T(8,128)(2,1)} custom-call(bf16[144,128,128]{2,1,0:T(8,128)(2,1)} %pack.5.out_ref), custom_call_target="tpu_custom_call" | custom-call | bytes 150994944 | tf_op jit(solution)/shard_map/exchange/pallas_call | solution.py:299
  206.7 16.0 %tiles.7 = f32[2048,512]{1,0:T(8,128)} custom-call(s32[256]{0:T(256)} %compare_select_fusion.12.pick_ref, s32[64]{0:T(128)S(1)} %copy-done.1, bf16[64,128,128]{2,1,0:T(8,128)(2,1)S(1)} %copy-done, bf16[64,128,128]{2,1,0:T(8,128)(2,1)} %collective-permute-done.b_ref.refs_1_, bf16[64,128,128]{2,1,0:T(8,128)(2,1)} %collective-permute-done.1.a_ref.refs_2_, ...), custom_call_target="tpu_custom_call" | custom-call | tf_op jit(solution)/shard_map/tiles/pallas_call | solution.py:191
  (30 shorter events, 0.2 us)
Async XLA Ops:
  0.0 30.7 %copy-start = (bf16[64,128,128]{2,1,0:T(8,128)(2,1)S(1)}, bf16[64,128,128]{2,1,0:T(8,128)(2,1)}, u32[]{:S(2)}) copy-start(bf16[64,128,128]{2,1,0:T(8,128)(2,1)} %refs_0_.1) | copy-start | bytes 6291460
  20.0 117.4 %collective-permute-start.1 = (bf16[64,128,128]{2,1,0:T(8,128)(2,1)}, bf16[64,128,128]{2,1,0:T(8,128)(2,1)}, u32[]{:S(2)}, u32[]{:S(2)}) collective-permute-start(bf16[64,128,128]{2,1,0:T(8,128)(2,1)} %refs_0_.1), channel_id=1, source_target_pairs={{0,16},{1,17},{2,18},{3,19},{4,20},{5,21},{6,22},{7,23},{8,24},{9,... | collective-permute-start | bytes 6291464 | tf_op jit(solution)/shard_map/ppermute | solution.py:324
  20.8 9.9 %collective-permute-start = (bf16[64,128,128]{2,1,0:T(8,128)(2,1)}, bf16[64,128,128]{2,1,0:T(8,128)(2,1)}, u32[]{:S(2)}, u32[]{:S(2)}) collective-permute-start(bf16[64,128,128]{2,1,0:T(8,128)(2,1)} %refs_0_.1), channel_id=1, source_target_pairs={{0,1},{1,0},{2,3},{3,2},{4,5},{5,4},{6,7},{7,6},{8,9},{9,8},{10,11... | collective-permute-start | bytes 6291464 | tf_op jit(solution)/shard_map/ppermute | solution.py:325
  137.4 5.0 %collective-permute-start.2 = (bf16[64,128,128]{2,1,0:T(8,128)(2,1)}, bf16[64,128,128]{2,1,0:T(8,128)(2,1)}, u32[]{:S(2)}, u32[]{:S(2)}) collective-permute-start(bf16[64,128,128]{2,1,0:T(8,128)(2,1)} %collective-permute-done.1.a_ref.refs_2_), channel_id=1, source_target_pairs={{0,1},{1,0},{2,3},{3,2},{4,5},{5,4},{6,7},{7,6},{8,9},{9,8},{10,11... | collective-permute-start | bytes 6291464 | tf_op jit(solution)/shard_map/ppermute | solution.py:332
  148.0 58.7 %copy-start.1 = (s32[64]{0:T(128)S(1)}, s32[64]{0:T(128)}, u32[]{:S(2)}) copy-start(s32[64]{0:T(128)} %read_ref.1) | copy-start | bytes 772
where the time goes:
time: 223 us
  Pallas kernels  205 us (92%)
  other arithmetic  9.12 us (4%)
  local copies, waits for them, and re-layouts  5.01 us (2%)
    pallas_call x2, Pallas kernels, exchange(): pl.pallas_call(functools.partial(exchange_kernel, devices, lane), out_sha...  160 us
    pallas_call x1, Pallas kernels, gather_rows(): pl.pallas_call(functools.partial(everyone_kernel, devices, group), out_sh...  17.9 us
    pallas_call x1, Pallas kernels, tiles(): pl.pallas_call(tile_kernel, out_shape=jax.ShapeDtypeStruct((RB_DEV * rows...  16 us
    pallas_call x2, Pallas kernels, pack(): pl.pallas_call(pack_kernel, out_shape=jax.ShapeDtypeStruct((send.shape[0]...  10.7 us
  transfers between devices with their start and end apart: 3, of which 0 were waited for; matrix products, arithmetic and copies ran while one was open for 6% of the time, Pallas kernels for 48%

commit v1 on v0

--- a/solution.py
+++ b/solution.py
@@ -108,7 +108,7 @@
         now = arrived - begin
         there = (part * half_devices + f * CORES + now % CORES) * lane + now // CORES + many
         there = jnp.where((now >= 0) & (now < lane * CORES), there, empty)
-        place = jnp.where(f == family, empty if local is None else local[None, :], there)
+        place = jnp.where((f == family) & (begin == 0), local[None, :], jnp.where(f == family, empty, there))
         place = place.reshape(families, HALVES, CORES * blocks).transpose(1, 0, 2).reshape(1, total)
         found = jnp.sum(jnp.where(match, place, 0), axis=1)
         return jnp.where(own > 0, found, empty)
@@ -116,38 +116,161 @@
     return send, pick, local
 
 
-def fill(near, held, sems):
-    blocks = near[0].shape[0]
-    copies = [
-        pltpu.make_async_copy(ref, held.at[pl.ds(i * blocks, blocks)], sems.at[i])
-        for i, ref in enumerate(near)
-    ]
-    for copy in copies:
-        copy.start()
+def lane_sizes(blocks, devices):
+    share = max(1, CORES * blocks * CORES // devices)
+    early, late = CORES * ((5 * share + 3) // 4), CORES * ((7 * share + 3) // 4)
+    kept = blocks // 4
+    cross = 4 * (CORES * (blocks - kept) // 5)
+    return early, late, kept, cross - cross % CORES
+
+
+def chip_counts(table, blocks, kept):
+    devices = lax.axis_size("dev")
+    chips = devices // CORES
+    source = jnp.where(table > 0, (table - 1) // (blocks * CORES), -1)
+    spot = (table - 1) % blocks
+    named = source[:, :, None] == iota(1, 1, chips, axis=2)
+    held = jnp.sum(i32(named), axis=0)
+    packed = jnp.sum(i32(named & (spot >= kept)[:, :, None]), axis=0)
+    return held, packed
+
+
+def too_full(table, blocks, early, late, kept, cross):
+    devices = lax.axis_size("dev")
+    chips = devices // CORES
+    families = devices // FAMILY
+    held, packed = chip_counts(table, blocks, kept)
+    here = (held > 0).astype(jnp.bfloat16)
+    demand = jnp.einsum(
+        "gc,gd->cd", held.astype(jnp.bfloat16), here, preferred_element_type=jnp.float32
+    )
+    c, d = iota(chips, chips, axis=0), iota(chips, chips, axis=1)
+    near = jnp.where(c // families == d // families, demand, 0.0)
+    far = jnp.where(c // families != d // families, demand, 0.0)
+    other = jnp.concatenate([far[families:], far[:families]], axis=0)
+    load = other + jnp.maximum(near - early, 0.0)
+    load = jnp.max(jnp.where(c % families != d % families, load, 0.0))
+    halves = jnp.max(here.reshape(-1, HALVES, families), axis=2)
+    crossing = jnp.einsum(
+        "gc,gh->ch", packed.astype(jnp.bfloat16), halves, preferred_element_type=jnp.float32
+    )
+    c, h = iota(chips, HALVES, axis=0), iota(chips, HALVES, axis=1)
+    crossing = jnp.max(jnp.where(c // families != h, crossing, 0.0))
+    return (load > late) | (crossing > cross)
+
+
+def plan(table, blocks, early, late, kept, cross):
+    devices = lax.axis_size("dev")
+    families = devices // FAMILY
+    many = FAMILY * blocks
+    pair = CORES * blocks
+    me = lax.axis_index("dev")
+    half, family, core = me // (devices // HALVES), me // CORES % families, me % CORES
+    part = np.repeat(np.arange(HALVES), pair)
+    x_core = np.tile(np.repeat(np.arange(CORES), blocks), HALVES)
+    x_block = np.tile(np.arange(blocks), FAMILY)
+    order = np.lexsort((x_block, x_core, (part == 1) & (x_block >= kept), part))
+    part, x_core, x_block = (jnp.asarray(v[order], jnp.int32) for v in (part, x_core, x_block))
+    x_half = jnp.where(half == 0, part, 1 - part)
+    away = jnp.where(core == 0, x_core, 1 - x_core)
+
+    ids = (((x_half * families + family) * CORES + x_core) * blocks + x_block + 1)[:, None]
+    inside = (table[0][None] == ids) | (table[1][None] == ids)
+    for j in range(2, CAP):
+        inside = inside | (table[j][None] == ids)
+    partners = jnp.stack(
+        [jnp.sum(jnp.where(inside, table[j][None], 0), axis=1) for j in range(CAP)]
+    )
+    chip = jnp.where(partners > 0, (partners - 1) // pair, -1)
+    f = iota(1, families, axis=1)
+    need = jnp.any(chip[:, :, None] == (f + half * families)[None], axis=0) & (f != family)
+    crosses = jnp.any((partners > 0) & (chip // families != x_half[None]), axis=0)
+    crosses = crosses & (x_block >= kept)
+    leaves, comes = crosses & (part == 0), crosses & (part == 1)
+    wide = jnp.concatenate([need, leaves[:, None], comes[:, None]], axis=1)
+    before = (iota(many, many, axis=1) < iota(many, many, axis=0)).astype(jnp.bfloat16)
+    ranks = i32(jnp.dot(before, wide.astype(jnp.bfloat16), preferred_element_type=jnp.float32))
+    ranks = jnp.where(wide, ranks, -1).T
+    rank, leaving, coming = ranks[:families], ranks[families], ranks[families + 1]
+    side = cross // CORES
+    second = i32(coming >= side)
+    packed = pair + CORES * kept
+    packed = packed + jnp.where(core == 0, second, 1 - second) * side + coming - second * side
+    local = jnp.where(
+        part == 0,
+        away * blocks + x_block,
+        jnp.where(x_block < kept, pair + away * kept + x_block, packed),
+    )
+
+    spots = iota(1, side, 1, axis=1)[0] + core * side
+    cross_send = jnp.sum(jnp.where(leaving[None] == spots, local[None], 0), axis=1)
+
+    def send(first, stop, lane):
+        spot = first[:, None, None] + iota(1, lane // CORES, 1, axis=1) + core * (lane // CORES)
+        hit = (rank[:, None, :] == spot) & (rank[:, None, :] < stop[:, None, None])
+        return jnp.sum(jnp.where(hit, local[None, None, :], 0), axis=2).reshape(-1)
+
+    zero = jnp.zeros((families,), jnp.int32)
+    near_count = jnp.sum(i32(need & (part == 0)[:, None]), axis=0)
+    shipped = jnp.minimum(near_count, early)
+    sends = send(zero, shipped, early), send(shipped, zero + many, late)
+
+    pairs = partners[:, :pair].reshape(-1)
+    all_ids = (
+        ((x_half[None] * families + iota(families, 1, axis=0)) * CORES + x_core[None]) * blocks
+        + x_block[None]
+        + 1
+    ).reshape(1, -1)
+    wanted = jnp.any(pairs[:, None] == all_ids, axis=0).reshape(families, many)
+    arrived = i32(
+        jnp.dot(wanted.astype(jnp.bfloat16), before.T, preferred_element_type=jnp.float32)
+    )
+    came = jnp.sum(i32(wanted & (part == 0)[None]), axis=1, keepdims=True)
+    came = jnp.minimum(came, early)
+    base = pair + CORES * kept + cross
+    g = iota(families, many, axis=0)
+    place = jnp.where(
+        arrived < came,
+        base + g * early + arrived,
+        base + families * early + g * late + arrived - came,
+    )
+    place = jnp.where(g == family, local[None], place).reshape(1, -1)
+    empty = base + families * (early + late)
+    own = lax.dynamic_slice(partners, (0, core * blocks), (CAP, blocks)).reshape(-1)
+    found = jnp.sum(jnp.where(own[:, None] == all_ids, place, 0), axis=1)
+    return cross_send, sends, jnp.where(own > 0, found, empty)
+
+
+def fill(refs, held, sems):
+    copies, at = [], 0
+    for i, ref in enumerate(refs):
+        copies.append(
+            pltpu.make_async_copy(ref, held.at[pl.ds(at, ref.shape[0])], sems.at[i])
+        )
+        copies[-1].start()
+        at += ref.shape[0]
     return copies
 
 
-def pack_kernel(send_ref, a_ref, b_ref, out_ref, held, sems):
-    for copy in fill((a_ref, b_ref), held, sems):
+def pack_kernel(parts, *refs):
+    sends, near = refs[:parts], refs[parts : -2 - parts]
+    outs, (held, sems) = refs[-2 - parts : -2], refs[-2:]
+    for copy in fill(near, held, sems):
         copy.wait()
-
-    def step(i, _):
-        out_ref[i] = held[send_ref[i]]
-        return 0
-
-    lax.fori_loop(0, out_ref.shape[0], step, 0, unroll=4)
+    for send_ref, out_ref in zip(sends, outs):
+
+        def step(i, _):
+            out_ref[i] = held[send_ref[i]]
+            return 0
+
+        lax.fori_loop(0, out_ref.shape[0], step, 0, unroll=2)
 
 
 def tile_kernel(pick_ref, read_ref, *refs):
-    near, got, (out_ref, held, sems) = refs[:FAMILY], refs[FAMILY:-3], refs[-3:]
+    near, (out_ref, held, sems) = refs[:-3], refs[-3:]
     blocks, rows = near[0].shape[:2]
-    base, many = FAMILY * blocks, got[0].shape[0]
     copies = fill(near, held, sems)
-    for i, ref in enumerate(got):
-        into = held.at[pl.ds(base + i * many, many)]
-        copies.append(pltpu.make_async_copy(ref, into, sems.at[FAMILY + i]))
-        copies[-1].start()
-    held[base + HALVES * many] = jnp.zeros(held.shape[1:], held.dtype)
+    held[held.shape[0] - 1] = jnp.zeros(held.shape[1:], held.dtype)
     out_ref[...] = jnp.zeros_like(out_ref)
     for copy in copies:
         copy.wait()
@@ -169,37 +292,40 @@
 VMEM = pl.BlockSpec(memory_space=pltpu.VMEM)
 
 
-def pack(send, near):
-    blocks, rows, kmers = near[0].shape
+def pack(sends, near):
+    rows, kmers = near[0].shape[1:]
+    total = sum(ref.shape[0] for ref in near)
     return pl.pallas_call(
-        pack_kernel,
-        out_shape=jax.ShapeDtypeStruct((send.shape[0], rows, kmers), near[0].dtype),
-        in_specs=[SMEM] + [HBM] * CORES,
-        out_specs=VMEM,
+        functools.partial(pack_kernel, len(sends)),
+        out_shape=[
+            jax.ShapeDtypeStruct((send.shape[0], rows, kmers), near[0].dtype) for send in sends
+        ],
+        in_specs=[SMEM] * len(sends) + [HBM] * len(near),
+        out_specs=[VMEM] * len(sends),
         scratch_shapes=[
-            pltpu.VMEM((CORES * blocks, rows, kmers), near[0].dtype),
-            pltpu.SemaphoreType.DMA((CORES,)),
+            pltpu.VMEM((total, rows, kmers), near[0].dtype),
+            pltpu.SemaphoreType.DMA((len(near),)),
         ],
         compiler_params=pltpu.CompilerParams(vmem_limit_bytes=60 << 20),
         name="pack",
-    )(send, *near)
-
-
-def tiles(pick, read_block, near, got):
-    blocks, rows, kmers = near[0].shape
-    total = FAMILY * blocks + HALVES * got[0].shape[0] + 1
+    )(*sends, *near)
+
+
+def tiles(pick, read_block, near):
+    rows, kmers = near[0].shape[1:]
+    total = sum(ref.shape[0] for ref in near) + 1
     return pl.pallas_call(
         tile_kernel,
         out_shape=jax.ShapeDtypeStruct((RB_DEV * rows, CAP * rows), jnp.float32),
-        in_specs=[SMEM, SMEM] + [HBM] * (FAMILY + HALVES),
+        in_specs=[SMEM, SMEM] + [HBM] * len(near),
         out_specs=VMEM,
         scratch_shapes=[
             pltpu.VMEM((total, rows, kmers), near[0].dtype),
-            pltpu.SemaphoreType.DMA((FAMILY + HALVES,)),
+            pltpu.SemaphoreType.DMA((len(near),)),
         ],
         compiler_params=pltpu.CompilerParams(vmem_limit_bytes=60 << 20),
         name="tiles",
-    )(pick, read_block, *near, *got)
+    )(pick, read_block, *near)
 
 
 def everyone_kernel(devices, group, row_ref, out_ref, send_sems, recv_sems):
@@ -310,38 +436,105 @@
     )(out)
 
 
+def swap_kernel(families, lane, out_ref, got_ref, send_sems, recv_sems, pass_sems, take_sems):
+    me = lax.axis_index("dev")
+    chip, core = me // CORES, me % CORES
+    spot = chip % families
+    side = lane // CORES
+
+    def copy_of(k):
+        to = flipped(spot, k)
+        return pltpu.make_async_remote_copy(
+            src_ref=out_ref.at[pl.ds(to * side, side)],
+            dst_ref=got_ref.at[pl.ds(spot * lane + core * side, side)],
+            send_sem=send_sems.at[k],
+            recv_sem=recv_sems.at[k],
+            device_id=((chip - spot + to) * CORES + core,),
+            device_id_type=pl.DeviceIdType.MESH,
+        )
+
+    def pass_of(k):
+        rows = got_ref.at[pl.ds(flipped(spot, k) * lane + core * side, side)]
+        return pltpu.make_async_remote_copy(
+            src_ref=rows,
+            dst_ref=rows,
+            send_sem=pass_sems.at[k],
+            recv_sem=take_sems.at[k],
+            device_id=(chip * CORES + 1 - core,),
+            device_id_type=pl.DeviceIdType.MESH,
+        )
+
+    masks = list(range(1, families))
+    copies = {k: copy_of(k) for k in masks}
+    passes = {k: pass_of(k) for k in masks}
+    for k in reversed(masks):
+        copies[k].start()
+    for k in masks:
+        copies[k].wait_recv()
+        passes[k].start()
+    for k in masks:
+        passes[k].wait_recv()
+    for k in masks:
+        copies[k].wait_send()
+        passes[k].wait_send()
+
+
+def swap_lanes(out, lane):
+    families = lax.axis_size("dev") // FAMILY
+    return pl.pallas_call(
+        functools.partial(swap_kernel, families, lane),
+        out_shape=jax.ShapeDtypeStruct((families * lane,) + out.shape[1:], out.dtype),
+        in_specs=[HBM],
+        out_specs=HBM,
+        scratch_shapes=[pltpu.SemaphoreType.DMA((families,))] * 4,
+        compiler_params=pltpu.CompilerParams(has_side_effects=True),
+        cost_estimate=pl.CostEstimate(
+            flops=0, bytes_accessed=32 * out.size * out.dtype.itemsize, transcendentals=0
+        ),
+        name="swap_lanes",
+    )(out)
+
+
 def shards(occurrence, block_owner, read_block, slot_order):
     devices = lax.axis_size("dev")
     blocks = occurrence.shape[0]
     slots = slot_order.shape[1]
-    lane = 2 * (2 * blocks // devices) + 1
     spill = 2 * blocks // devices
+    early, late, kept, cross = lane_sizes(blocks, devices)
     swap = [(d, d ^ 1) for d in range(devices)]
     across = [(d, (d + devices // HALVES) % devices) for d in range(devices)]
     row = jnp.stack([jnp.pad(block_owner[:, 0], (0, slots - blocks)), slot_order[0]])
     everyone = gather_rows(row)
     everyone, mine = lax.optimization_barrier((everyone, occurrence))
-    far = lax.ppermute(mine, "dev", across)
+    far = lax.ppermute(mine[:kept], "dev", across)
     sibling = lax.ppermute(mine, "dev", swap)
     table = group_table(everyone[:, 0, :blocks], everyone[:, 1])
-    most = i32(fullest_lane(table, blocks))
-    send, pick, local = routes(table, blocks)
-    begin = CORES * lane
-    got = exchange(pack(send(0, lane, False), (occurrence, sibling)), lane)
-    far, got = lax.optimization_barrier((far, got))
-    distant = (far, lax.ppermute(far, "dev", swap))
-    near = (occurrence, sibling) + distant
-    also = exchange(pack(send(0, lane, True), distant), lane)
-    first = tiles(pick(0, lane, local), read_block, near, (got, also))
+    cross_send, sends, pick = plan(table, blocks, early, late, kept, cross)
+    full = too_full(table, blocks, early, late, kept, cross)
+    crossing, out = pack((cross_send, sends[0]), (mine, sibling))
+    crossed = lax.ppermute(crossing, "dev", across)
+    got = swap_lanes(out, early)
+    far, crossed, got = lax.optimization_barrier((far, crossed, got))
+    near = (mine, sibling, far, lax.ppermute(far, "dev", swap))
+    near = near + (crossed, lax.ppermute(crossed, "dev", swap))
+    also = swap_lanes(pack((sends[1],), near)[0], late)
+    first = tiles(pick, read_block, near + (got, also))
 
     def more(carry):
-        begin, margin = carry
-        got = exchange(pack(send(begin, spill, False), near[:CORES]), spill)
-        also = exchange(pack(send(begin, spill, True), distant), spill)
-        added = tiles(pick(begin, spill, None), read_block, near, (got, also))
-        return begin + CORES * spill, margin + added
-
-    return lax.while_loop(lambda carry: carry[0] < most, more, (jnp.int32(begin), first))[1]
+        begin, stop, margin = carry
+        begin, now, mine = lax.optimization_barrier((begin, table, occurrence))
+        send, pick, local = routes(now, blocks)
+        sibling = lax.ppermute(mine, "dev", swap)
+        far = lax.ppermute(mine, "dev", across)
+        near = (mine, sibling, far, lax.ppermute(far, "dev", swap))
+        got = exchange(pack((send(begin, spill, False),), near[:CORES])[0], spill)
+        also = exchange(pack((send(begin, spill, True),), near[CORES:])[0], spill)
+        added = tiles(pick(begin, spill, local), read_block, near + (got, also))
+        margin = jnp.where(begin == 0, 0.0, margin) + added
+        return begin + CORES * spill, i32(fullest_lane(now, blocks)), margin
+
+    start = jnp.int32(0), jnp.where(full, 1, 0).astype(jnp.int32), first
+    return lax.while_loop(lambda carry: carry[0] < carry[1], more, start)[2]
 
 
 def solution(mesh):

time: 223 us -> 204 us (0.915)
  Pallas kernels: 205 us -> 177 us
  other arithmetic: 9.12 us -> 12.7 us
  starting transfers between devices: 1.26 us -> 3.69 us
    pallas_call x4, Pallas kernels: 171 us -> 142 us  [the longest x2 131 us: swap_lanes(): pl.pallas_call(functools.partial(swap_kernel, families, lane), out_shape=...]
    ppermute x2 -> x4, starting transfers between devices: 1.26 us -> 3.61 us  [the longest x1 2.26 us: shards(): crossed = lax.ppermute(crossing, 'dev', across)]
  transfers between devices with their start and end apart: 3 -> 5, of which waited for: 0 -> 0; matrix products, arithmetic and copies ran while one was open for 6% -> 9% of each run, Pallas kernels for 48% -> 38%
where the time goes in v1:
time: 204 us; the launch traced here: 203 us
  Pallas kernels  177 us (87%)
  other arithmetic  12.7 us (6%)
  local copies, waits for them, and re-layouts  6.85 us (3%)
  starting transfers between devices  3.69 us (2%)
    pallas_call x2, Pallas kernels, swap_lanes(): pl.pallas_call(functools.partial(swap_kernel, families, lane), out_shape=...  131 us
    pallas_call x1, Pallas kernels, gather_rows(): pl.pallas_call(functools.partial(everyone_kernel, devices, group), out_sh...  18 us
    pallas_call x1, Pallas kernels, tiles(): pl.pallas_call(tile_kernel, out_shape=jax.ShapeDtypeStruct((RB_DEV * rows...  16.7 us
    pallas_call x2, Pallas kernels, pack(): pl.pallas_call(functools.partial(pack_kernel, len(sends)), out_shape=[jax...  10.7 us
  transfers between devices with their start and end apart: 5, of which 0 were waited for; matrix products, arithmetic and copies ran while one was open for 9% of the time, Pallas kernels for 38%

profile of v1, /device:TPU:0, one launch (start us, length us, event | category | flops | bytes accessed | tf_op | source)
XLA Modules:
  0.0 203.1 jit_solution(1936726151118855663)
XLA Ops:
  0.1 0.8 pad_bitcast_fusion
  0.9 1.2 pad_add_fusion.2.row_ref
  2.1 18.0 %gather_rows.1 = s32[32,2,128]{2,1,0:T(2,128)} custom-call(s32[2,128]{1,0:T(2,128)} %pad_add_fusion.2.row_ref), custom_call_target="tpu_custom_call" | custom-call | tf_op jit(solution)/shard_map/gather_rows/pallas_call | solution.py:366
  20.1 0.1 collective-permute-start.3
  20.1 1.9 slice.89
  22.0 0.7 collective-permute-start.4
  22.8 0.8 slice.80
  23.6 0.8 slice.79
  24.4 0.7 broadcast_select_fusion.2
  25.1 0.7 add_bitcast_fusion
  25.8 0.9 convert_reduce_fusion.1
  26.8 0.1 add_add_fusion.2
  26.8 0.7 select_reduce_fusion.12
  27.5 0.1 copy.21
  27.6 0.1 copy.22
  27.8 0.1 copy.19
  27.9 0.1 copy.20
  28.0 2.9 %select_reduce_fusion.7 = s32[4,32,32]{2,1,0:T(8,128)S(1)} fusion(s32[32,128]{1,0:T(8,128)S(1)} %copy.23, s32[4,32,32]{2,1,0:T(8,128)S(1)} %copy.20), kind=kLoop, calls=%fused_computation.131 | loop fusion | flops 1568768 | bytes 49152 | tf_op jit(solution)/shard_map/reduce_sum | solution.py:39
  31.2 0.9 select_reduce_fusion.11
  32.2 0.1 compare_reduce_fusion.3
  32.3 0.2 convert_reduce_fusion.4
  32.5 0.7 compare_reduce_fusion.2
  33.2 0.1 reshape.651
  33.3 0.2 fusion.50
  33.7 0.3 select_reduce_fusion.14
  34.0 0.1 copy.24
  34.1 0.7 reshape.654.refs_1_
  34.8 0.1 convert_reduce_fusion.5
  35.0 0.8 select_reduce_fusion.15.refs_0_
  35.8 4.9 %pack.4 = (bf16[38,128,128]{2,1,0:T(8,128)(2,1)}, bf16[80,128,128]{2,1,0:T(8,128)(2,1)}) custom-call(s32[38]{0:T(128)} %select_reduce_fusion.15.refs_0_, s32[80]{0:T(128)} %reshape.654.refs_1_, bf16[64,128,128]{2,1,0:T(8,128)(2,1)S(1)} %copy-done, bf16[64,128,128]{2,1,0:T(8,128)(2,1)} %collective-permute-done.3.refs_3_.refs_2_.refs_1_), custom_call_target="tpu_custom_call" | custom-call | tf_op jit(solution)/shard_map/pack/pallas_call | solution.py:298
  40.6 2.3 %collective-permute-start.5 = (bf16[38,128,128]{2,1,0:T(8,128)(2,1)}, bf16[38,128,128]{2,1,0:T(8,128)(2,1)S(1)}, u32[]{:S(2)}, u32[]{:S(2)}) collective-permute-start(bf16[38,128,128]{2,1,0:T(8,128)(2,1)} %get-tuple-element.153), channel_id=1, source_target_pairs={{0,16},{1,17},{2,18},{3,19},{4,20},{5,21},{6,22},{7,23},{8,24},{9,... | collective-permute-start | bytes 3735560 | tf_op jit(solution)/shard_map/ppermute | solution.py:515
  43.0 0.8 fusion.51
  43.8 0.4 select_reduce_fusion.13
  44.2 71.6 %swap_lanes.2.refs_6_ = bf16[160,128,128]{2,1,0:T(8,128)(2,1)} custom-call(bf16[80,128,128]{2,1,0:T(8,128)(2,1)} %get-tuple-element.154.out_ref), custom_call_target="tpu_custom_call" | custom-call | bytes 83886080 | tf_op jit(solution)/shard_map/swap_lanes/pallas_call | solution.py:484
  115.9 0.5 collective-permute-start.7
  116.4 0.2 select_bitcast_fusion
  116.5 0.1 fusion.67
  116.7 0.2 collective-permute-start.6
  116.8 0.1 reshape.652
  116.9 0.1 copy.25
  117.0 0.7 reshape.655.refs_0_
  118.3 0.7 fusion.66
  119.7 0.3 select_reduce_fusion.6
  120.0 0.6 compare_select_fusion.11.pick_ref
  120.6 5.8 %pack.5.out_ref = bf16[112,128,128]{2,1,0:T(8,128)(2,1)} custom-call(s32[112]{0:T(128)} %reshape.655.refs_0_, bf16[64,128,128]{2,1,0:T(8,128)(2,1)S(1)} %copy-done, bf16[64,128,128]{2,1,0:T(8,128)(2,1)} %collective-permute-done.3.refs_3_.refs_2_.refs_1_, bf16[16,128,128]{2,1,0:T(8,128)(2,1)} %collective-permute-done.4.refs_3_.refs_2_, ...), custom_call_target="tpu_custom_call" | custom-call | tf_op jit(solution)/shard_map/pack/pallas_call | solution.py:298
  126.5 59.5 %swap_lanes.3.refs_7_ = bf16[224,128,128]{2,1,0:T(8,128)(2,1)} custom-call(bf16[112,128,128]{2,1,0:T(8,128)(2,1)} %pack.5.out_ref), custom_call_target="tpu_custom_call" | custom-call | bytes 117440512 | tf_op jit(solution)/shard_map/swap_lanes/pallas_call | solution.py:484
  186.0 16.7 %tiles.6 = f32[2048,512]{1,0:T(8,128)} custom-call(s32[256]{0:T(256)} %compare_select_fusion.11.pick_ref, s32[64]{0:T(128)S(1)} %copy-done.2, bf16[64,128,128]{2,1,0:T(8,128)(2,1)S(1)} %copy-done, bf16[64,128,128]{2,1,0:T(8,128)(2,1)} %collective-permute-done.3.refs_3_.refs_2_.refs_1_, bf16[16,128,128]{2,1,0:T(8,128)(2,1)} %collective-permute-done.4.refs_3_.refs_2_, ...), custom_call_target="tpu_custom_call" | custom-call | tf_op jit(solution)/shard_map/tiles/pallas_call | solution.py:317
  202.7 0.2 while.15
  (63 shorter events, 0.9 us)
Async XLA Ops:
  0.0 33.5 %copy-start.3 = (s32[256]{0:T(256)S(1)}, s32[256]{0:T(256)}, u32[]{:S(2)}) copy-start(s32[256]{0:T(256)} %constant.621.clone) | copy-start | bytes 3076
  0.0 33.6 %copy-start.4 = (s32[256]{0:T(256)S(1)}, s32[256]{0:T(256)}, u32[]{:S(2)}) copy-start(s32[256]{0:T(256)} %constant.620.clone) | copy-start | bytes 3076
  0.0 32.3 %copy-start.5 = (pred[256]{0:T(512)(128)(4,1)S(1)}, pred[256]{0:T(512)(128)(4,1)}, u32[]{:S(2)}) copy-start(pred[256]{0:T(512)(128)(4,1)} %constant.627) | copy-start | bytes 772
  0.0 32.5 %copy-start.7 = (pred[256]{0:T(512)(128)(4,1)S(1)}, pred[256]{0:T(512)(128)(4,1)}, u32[]{:S(2)}) copy-start(pred[256]{0:T(512)(128)(4,1)} %constant.632) | copy-start | bytes 772
  0.0 32.5 %copy-start.8 = (pred[256]{0:T(512)(128)(4,1)S(1)}, pred[256]{0:T(512)(128)(4,1)}, u32[]{:S(2)}) copy-start(pred[256]{0:T(512)(128)(4,1)} %constant.631) | copy-start | bytes 772
  0.0 33.6 %copy-start.9 = (pred[256]{0:T(512)(128)(4,1)S(1)}, pred[256]{0:T(512)(128)(4,1)}, u32[]{:S(2)}) copy-start(pred[256]{0:T(512)(128)(4,1)} %constant.630) | copy-start | bytes 772
  0.0 33.6 %copy-start.6 = (s32[256]{0:T(256)S(1)}, s32[256]{0:T(256)}, u32[]{:S(2)}) copy-start(s32[256]{0:T(256)} %constant.629) | copy-start | bytes 3076
  0.0 35.7 %copy-start = (bf16[64,128,128]{2,1,0:T(8,128)(2,1)S(1)}, bf16[64,128,128]{2,1,0:T(8,128)(2,1)}, u32[]{:S(2)}) copy-start(bf16[64,128,128]{2,1,0:T(8,128)(2,1)} %refs_0_) | copy-start | bytes 6291460
  20.1 15.7 %collective-permute-start.3 = (bf16[64,128,128]{2,1,0:T(8,128)(2,1)}, bf16[64,128,128]{2,1,0:T(8,128)(2,1)}, u32[]{:S(2)}, u32[]{:S(2)}) collective-permute-start(bf16[64,128,128]{2,1,0:T(8,128)(2,1)} %refs_0_), channel_id=1, source_target_pairs={{0,1},{1,0},{2,3},{3,2},{4,5},{5,4},{6,7},{7,6},{8,9},{9,8},{10,11... | collective-permute-start | bytes 6291464 | tf_op jit(solution)/shard_map/ppermute | solution.py:510
  22.0 93.8 %collective-permute-start.4 = (bf16[16,128,128]{2,1,0:T(8,128)(2,1)}, bf16[16,128,128]{2,1,0:T(8,128)(2,1)}, u32[]{:S(2)}, u32[]{:S(2)}) collective-permute-start(bf16[16,128,128]{2,1,0:T(8,128)(2,1)} %slice.89), channel_id=1, source_target_pairs={{0,16},{1,17},{2,18},{3,19},{4,20},{5,21},{6,22},{7,23},{8,24},{9,... | collective-permute-start | bytes 1572872 | tf_op jit(solution)/shard_map/ppermute | solution.py:509
  40.6 75.3 %collective-permute-start.5 = (bf16[38,128,128]{2,1,0:T(8,128)(2,1)}, bf16[38,128,128]{2,1,0:T(8,128)(2,1)S(1)}, u32[]{:S(2)}, u32[]{:S(2)}) collective-permute-start(bf16[38,128,128]{2,1,0:T(8,128)(2,1)} %get-tuple-element.153), channel_id=1, source_target_pairs={{0,16},{1,17},{2,18},{3,19},{4,20},{5,21},{6,22},{7,23},{8,24},{9,... | collective-permute-start | bytes 3735560 | tf_op jit(solution)/shard_map/ppermute | solution.py:515
  115.9 4.7 %copy-start.1 = (bf16[38,128,128]{2,1,0:T(8,128)(2,1)}, bf16[38,128,128]{2,1,0:T(8,128)(2,1)S(1)}, u32[]{:S(2)}) copy-start(bf16[38,128,128]{2,1,0:T(8,128)(2,1)S(1)} %collective-permute-done.5.refs_5_.refs_4_) | copy-start | bytes 3735556
  115.9 4.7 %collective-permute-start.7 = (bf16[38,128,128]{2,1,0:T(8,128)(2,1)S(1)}, bf16[38,128,128]{2,1,0:T(8,128)(2,1)}, u32[]{:S(2)}, u32[]{:S(2)}) collective-permute-start(bf16[38,128,128]{2,1,0:T(8,128)(2,1)S(1)} %collective-permute-done.5.refs_5_.refs_4_), channel_id=1, source_target_pairs={{0,1},{1,0},{2,3},{3,2},{4,5},{5,4},{6,7},{7,6},{8,9},{9,8},{10,11... | collective-permute-start | bytes 3735560 | tf_op jit(solution)/shard_map/ppermute | solution.py:519
  116.7 3.9 %collective-permute-start.6 = (bf16[16,128,128]{2,1,0:T(8,128)(2,1)}, bf16[16,128,128]{2,1,0:T(8,128)(2,1)}, u32[]{:S(2)}, u32[]{:S(2)}) collective-permute-start(bf16[16,128,128]{2,1,0:T(8,128)(2,1)} %collective-permute-done.4.refs_3_.refs_2_), channel_id=1, source_target_pairs={{0,1},{1,0},{2,3},{3,2},{4,5},{5,4},{6,7},{7,6},{8,9},{9,8},{10,11... | collective-permute-start | bytes 1572872 | tf_op jit(solution)/shard_map/ppermute | solution.py:518
  126.5 59.5 %copy-start.2 = (s32[64]{0:T(128)S(1)}, s32[64]{0:T(128)}, u32[]{:S(2)}) copy-start(s32[64]{0:T(128)} %read_ref.1) | copy-start | bytes 772

commit v2 on v1

--- a/solution.py
+++ b/solution.py
@@ -12,6 +12,8 @@
 CORES = 2
 HALVES = 2
 FAMILY = CORES * HALVES
+AHEAD = 2
+TOGETHER = 4
 
 
 def i32(x):
@@ -275,16 +277,22 @@
     for copy in copies:
         copy.wait()
 
-    def step(b, _):
+    def tile_of(b):
         others = jnp.concatenate([held[pick_ref[j * blocks + b]] for j in range(CAP)], axis=0)
         tile = lax.dot_general(
             held[b], others, (((1,), (1,)), ((), ())), preferred_element_type=jnp.float32
         )
-        where = pl.ds(pl.multiple_of(read_ref[b] * rows, rows), rows)
-        out_ref[where, :] += tile.astype(jnp.bfloat16).astype(jnp.float32)
+        return tile.astype(jnp.bfloat16)
+
+    def step(i, _):
+        found = [tile_of(i * TOGETHER + k) for k in range(TOGETHER)]
+        for k in range(TOGETHER):
+            begin = read_ref[i * TOGETHER + k] * rows
+            where = pl.ds(pl.multiple_of(begin, rows), rows)
+            out_ref[where, :] += found[k].astype(jnp.float32)
         return 0
 
-    lax.fori_loop(0, blocks, step, 0, unroll=2)
+    lax.fori_loop(0, blocks // TOGETHER, step, 0, unroll=2)
 
 
 SMEM = pl.BlockSpec(memory_space=pltpu.SMEM)
@@ -328,48 +336,45 @@
     )(pick, read_block, *near)
 
 
-def everyone_kernel(devices, group, row_ref, out_ref, send_sems, recv_sems):
+def greet(others):
+    barrier = pltpu.get_barrier_semaphore()
+    for other in others:
+        pl.semaphore_signal(
+            barrier, inc=1, device_id=(other,), device_id_type=pl.DeviceIdType.MESH
+        )
+    pl.semaphore_wait(barrier, len(others))
+
+
+def everyone_kernel(devices, row_ref, out_ref, send_sems, recv_sems):
     me = lax.axis_index("dev")
-    first = me // group * group
     out_ref[me] = row_ref[...]
-
-    def spread(src, dst, to, k):
-        copy = pltpu.make_async_remote_copy(
-            src_ref=src,
-            dst_ref=dst,
+    greet([(me + k) % devices for k in range(1, devices)])
+    copies = [
+        pltpu.make_async_remote_copy(
+            src_ref=row_ref,
+            dst_ref=out_ref.at[me],
             send_sem=send_sems.at[k],
             recv_sem=recv_sems.at[k],
-            device_id=(to,),
+            device_id=((me + k) % devices,),
             device_id_type=pl.DeviceIdType.MESH,
         )
+        for k in range(1, devices)
+    ]
+    for copy in copies:
         copy.start()
-        return copy
-
-    near = [
-        spread(row_ref, out_ref.at[me], first + (me - first + k) % group, k)
-        for k in range(1, group)
-    ]
-    for copy in near:
+    for copy in copies:
         copy.wait()
-    rows = out_ref.at[pl.ds(first, group)]
-    far = [
-        spread(rows, rows, (me + k * group) % devices, group + k)
-        for k in range(1, devices // group)
-    ]
-    for copy in far:
-        copy.wait()
 
 
 def gather_rows(row):
     devices = lax.axis_size("dev")
-    group = 1 << devices.bit_length() // 2
     return pl.pallas_call(
-        functools.partial(everyone_kernel, devices, group),
+        functools.partial(everyone_kernel, devices),
         out_shape=jax.ShapeDtypeStruct((devices,) + row.shape, row.dtype),
         in_specs=[VMEM],
         out_specs=VMEM,
-        scratch_shapes=[pltpu.SemaphoreType.DMA((group + devices // group,))] * 2,
-        compiler_params=pltpu.CompilerParams(has_side_effects=True),
+        scratch_shapes=[pltpu.SemaphoreType.DMA((devices,))] * 2,
+        compiler_params=pltpu.CompilerParams(has_side_effects=True, collective_id=0),
         name="gather_rows",
     )(row)
 
@@ -464,22 +469,29 @@
             device_id_type=pl.DeviceIdType.MESH,
         )
 
-    masks = list(range(1, families))
-    copies = {k: copy_of(k) for k in masks}
-    passes = {k: pass_of(k) for k in masks}
-    for k in reversed(masks):
-        copies[k].start()
-    for k in masks:
-        copies[k].wait_recv()
-        passes[k].start()
-    for k in masks:
-        passes[k].wait_recv()
-    for k in masks:
-        copies[k].wait_send()
-        passes[k].wait_send()
-
-
-def swap_lanes(out, lane):
+    chips = [(chip - spot + flipped(spot, k)) * CORES + core for k in range(1, families)]
+    greet(chips + [chip * CORES + 1 - core])
+    top = families - 1
+    steps = [[k for k in (m, top - m) if k] for m in range(top, families // 2 - 1, -1)]
+    copies = [[copy_of(k) for k in step] for step in steps]
+    passes = [[pass_of(k) for k in step] for step in steps]
+    for i in range(len(steps) + AHEAD):
+        if i >= AHEAD:
+            for copy in copies[i - AHEAD]:
+                copy.wait_send()
+        if i < len(steps):
+            for copy in copies[i]:
+                copy.start()
+        if i >= AHEAD:
+            for copy, follow in zip(copies[i - AHEAD], passes[i - AHEAD]):
+                copy.wait_recv()
+                follow.start()
+    for step in passes:
+        for follow in step:
+            follow.wait()
+
+
+def swap_lanes(out, lane, number):
     families = lax.axis_size("dev") // FAMILY
     return pl.pallas_call(
         functools.partial(swap_kernel, families, lane),
@@ -487,7 +499,7 @@
         in_specs=[HBM],
         out_specs=HBM,
         scratch_shapes=[pltpu.SemaphoreType.DMA((families,))] * 4,
-        compiler_params=pltpu.CompilerParams(has_side_effects=True),
+        compiler_params=pltpu.CompilerParams(has_side_effects=True, collective_id=number),
         cost_estimate=pl.CostEstimate(
             flops=0, bytes_accessed=32 * out.size * out.dtype.itemsize, transcendentals=0
         ),
@@ -513,11 +525,11 @@
     full = too_full(table, blocks, early, late, kept, cross)
     crossing, out = pack((cross_send, sends[0]), (mine, sibling))
     crossed = lax.ppermute(crossing, "dev", across)
-    got = swap_lanes(out, early)
+    got = swap_lanes(out, early, 1)
     far, crossed, got = lax.optimization_barrier((far, crossed, got))
     near = (mine, sibling, far, lax.ppermute(far, "dev", swap))
     near = near + (crossed, lax.ppermute(crossed, "dev", swap))
-    also = swap_lanes(pack((sends[1],), near)[0], late)
+    also = swap_lanes(pack((sends[1],), near)[0], late, 2)
     first = tiles(pick, read_block, near + (got, also))
 
     def more(carry):

time: 204 us -> 176 us (0.86)
  Pallas kernels: 177 us -> 149 us
    pallas_call x2, Pallas kernels: 131 us -> 115 us  [swap_lanes(): pl.pallas_call(functools.partial(swap_kernel, families, lane), out_shape=...]
    pallas_call x1, Pallas kernels: 18 us -> 11.2 us  [gather_rows(): pl.pallas_call(functools.partial(everyone_kernel, devices), out_shape=jax...]
    pallas_call x1, Pallas kernels: 16.7 us -> 12.7 us  [tiles(): pl.pallas_call(tile_kernel, out_shape=jax.ShapeDtypeStruct((RB_DEV * rows...]
  transfers between devices with their start and end apart: 5 -> 5, of which waited for: 0 -> 0; matrix products, arithmetic and copies ran while one was open for 9% -> 11% of each run, Pallas kernels for 38% -> 41%
where the time goes in v2:
time: 176 us
  Pallas kernels  149 us (85%)
  other arithmetic  12.7 us (7%)
  local copies, waits for them, and re-layouts  6.85 us (4%)
  starting transfers between devices  3.79 us (2%)
  between operations  1.86 us (1%)
    pallas_call x2, Pallas kernels, swap_lanes(): pl.pallas_call(functools.partial(swap_kernel, families, lane), out_shape=...  115 us
    pallas_call x1, Pallas kernels, tiles(): pl.pallas_call(tile_kernel, out_shape=jax.ShapeDtypeStruct((RB_DEV * rows...  12.7 us
    pallas_call x1, Pallas kernels, gather_rows(): pl.pallas_call(functools.partial(everyone_kernel, devices), out_shape=jax...  11.2 us
    pallas_call x2, Pallas kernels, pack(): pl.pallas_call(functools.partial(pack_kernel, len(sends)), out_shape=[jax...  10.7 us
  transfers between devices with their start and end apart: 5, of which 0 were waited for; matrix products, arithmetic and copies ran while one was open for 11% of the time, Pallas kernels for 41%

profile of v2, /device:TPU:0, one launch (start us, length us, event | category | flops | bytes accessed | tf_op | source)
XLA Modules:
  0.0 175.9 jit_solution(16995253113395531064)
XLA Ops:
  0.1 0.8 pad_bitcast_fusion
  0.9 1.2 pad_add_fusion.2.row_ref
  2.1 11.2 %gather_rows.1 = s32[32,2,128]{2,1,0:T(2,128)} custom-call(s32[2,128]{1,0:T(2,128)} %pad_add_fusion.2.row_ref), custom_call_target="tpu_custom_call" | custom-call | tf_op jit(solution)/shard_map/gather_rows/pallas_call | solution.py:371
  13.3 0.2 collective-permute-start.3
  13.4 1.9 %slice.89 = bf16[16,128,128]{2,1,0:T(8,128)(2,1)} slice(bf16[64,128,128]{2,1,0:T(8,128)(2,1)} %refs_0_), slice={[0:16], [0:128], [0:128]} | slice | bytes 1048576 | tf_op jit(solution)/shard_map/slice | solution.py:521
  15.3 2.3 %collective-permute-start.4 = (bf16[16,128,128]{2,1,0:T(8,128)(2,1)}, bf16[16,128,128]{2,1,0:T(8,128)(2,1)}, u32[]{:S(2)}, u32[]{:S(2)}) collective-permute-start(bf16[16,128,128]{2,1,0:T(8,128)(2,1)} %slice.89), channel_id=1, source_target_pairs={{0,16},{1,17},{2,18},{3,19},{4,20},{5,21},{6,22},{7,23},{8,24},{9,... | collective-permute-start | bytes 1572872 | tf_op jit(solution)/shard_map/ppermute | solution.py:521
  17.7 0.8 slice.80
  18.4 0.8 slice.79
  19.2 0.7 broadcast_select_fusion.2
  20.0 0.7 add_bitcast_fusion
  20.7 0.9 convert_reduce_fusion.1
  21.6 0.1 add_add_fusion.2
  21.7 0.7 select_reduce_fusion.12
  22.4 0.1 copy.21
  22.5 0.1 copy.22
  22.7 0.1 copy.19
  22.8 0.1 copy.20
  22.9 2.9 %select_reduce_fusion.7 = s32[4,32,32]{2,1,0:T(8,128)S(1)} fusion(s32[32,128]{1,0:T(8,128)S(1)} %copy.23, s32[4,32,32]{2,1,0:T(8,128)S(1)} %copy.20), kind=kLoop, calls=%fused_computation.131 | loop fusion | flops 1568768 | bytes 49152 | tf_op jit(solution)/shard_map/reduce_sum | solution.py:41
  26.1 0.9 select_reduce_fusion.11
  27.1 0.1 compare_reduce_fusion.3
  27.2 0.2 convert_reduce_fusion.4
  27.4 0.7 compare_reduce_fusion.2
  28.0 0.1 reshape.651
  28.2 0.2 fusion.50
  28.5 0.3 select_reduce_fusion.14
  28.9 0.1 copy.24
  28.9 0.7 reshape.654.refs_1_
  29.7 0.1 convert_reduce_fusion.5
  29.8 0.8 select_reduce_fusion.15.refs_0_
  30.6 4.9 %pack.4 = (bf16[38,128,128]{2,1,0:T(8,128)(2,1)}, bf16[80,128,128]{2,1,0:T(8,128)(2,1)}) custom-call(s32[38]{0:T(128)} %select_reduce_fusion.15.refs_0_, s32[80]{0:T(128)} %reshape.654.refs_1_, bf16[64,128,128]{2,1,0:T(8,128)(2,1)S(1)} %copy-done, bf16[64,128,128]{2,1,0:T(8,128)(2,1)} %collective-permute-done.3.refs_3_.refs_2_.refs_1_), custom_call_target="tpu_custom_call" | custom-call | tf_op jit(solution)/shard_map/pack/pallas_call | solution.py:306
  35.5 0.7 collective-permute-start.5
  36.3 0.8 fusion.51
  37.1 0.4 select_reduce_fusion.13
  37.5 67.2 %swap_lanes.2.refs_6_ = bf16[160,128,128]{2,1,0:T(8,128)(2,1)} custom-call(bf16[80,128,128]{2,1,0:T(8,128)(2,1)} %get-tuple-element.154.out_ref), custom_call_target="tpu_custom_call" | custom-call | bytes 83886080 | tf_op jit(solution)/shard_map/swap_lanes/pallas_call | solution.py:496
  104.8 0.4 collective-permute-start.7
  105.2 0.2 select_bitcast_fusion
  105.4 0.1 fusion.67
  105.6 0.2 collective-permute-start.6
  105.7 0.1 reshape.652
  105.8 0.1 copy.25
  105.9 0.7 reshape.655.refs_0_
  107.2 0.7 fusion.66
  108.6 0.3 select_reduce_fusion.6
  108.9 0.6 compare_select_fusion.11.pick_ref
  109.5 5.8 %pack.5.out_ref = bf16[112,128,128]{2,1,0:T(8,128)(2,1)} custom-call(s32[112]{0:T(128)} %reshape.655.refs_0_, bf16[64,128,128]{2,1,0:T(8,128)(2,1)S(1)} %copy-done, bf16[64,128,128]{2,1,0:T(8,128)(2,1)} %collective-permute-done.3.refs_3_.refs_2_.refs_1_, bf16[16,128,128]{2,1,0:T(8,128)(2,1)} %collective-permute-done.4.refs_3_.refs_2_, ...), custom_call_target="tpu_custom_call" | custom-call | tf_op jit(solution)/shard_map/pack/pallas_call | solution.py:306
  115.4 47.5 %swap_lanes.3.refs_7_ = bf16[224,128,128]{2,1,0:T(8,128)(2,1)} custom-call(bf16[112,128,128]{2,1,0:T(8,128)(2,1)} %pack.5.out_ref), custom_call_target="tpu_custom_call" | custom-call | bytes 117440512 | tf_op jit(solution)/shard_map/swap_lanes/pallas_call | solution.py:496
  162.9 12.7 %tiles.6 = f32[2048,512]{1,0:T(8,128)} custom-call(s32[256]{0:T(256)} %compare_select_fusion.11.pick_ref, s32[64]{0:T(128)S(1)} %copy-done.2, bf16[64,128,128]{2,1,0:T(8,128)(2,1)S(1)} %copy-done, bf16[64,128,128]{2,1,0:T(8,128)(2,1)} %collective-permute-done.3.refs_3_.refs_2_.refs_1_, bf16[16,128,128]{2,1,0:T(8,128)(2,1)} %collective-permute-done.4.refs_3_.refs_2_, ...), custom_call_target="tpu_custom_call" | custom-call | tf_op jit(solution)/shard_map/tiles/pallas_call | solution.py:325
  175.6 0.2 while.15
  (63 shorter events, 0.9 us)
Async XLA Ops:
  0.0 28.4 %copy-start.3 = (s32[256]{0:T(256)S(1)}, s32[256]{0:T(256)}, u32[]{:S(2)}) copy-start(s32[256]{0:T(256)} %constant.621.clone) | copy-start | bytes 3076
  0.0 28.4 %copy-start.4 = (s32[256]{0:T(256)S(1)}, s32[256]{0:T(256)}, u32[]{:S(2)}) copy-start(s32[256]{0:T(256)} %constant.620.clone) | copy-start | bytes 3076
  0.0 27.2 %copy-start.5 = (pred[256]{0:T(512)(128)(4,1)S(1)}, pred[256]{0:T(512)(128)(4,1)}, u32[]{:S(2)}) copy-start(pred[256]{0:T(512)(128)(4,1)} %constant.627) | copy-start | bytes 772
  0.0 27.3 %copy-start.7 = (pred[256]{0:T(512)(128)(4,1)S(1)}, pred[256]{0:T(512)(128)(4,1)}, u32[]{:S(2)}) copy-start(pred[256]{0:T(512)(128)(4,1)} %constant.632) | copy-start | bytes 772
  0.0 27.4 %copy-start.8 = (pred[256]{0:T(512)(128)(4,1)S(1)}, pred[256]{0:T(512)(128)(4,1)}, u32[]{:S(2)}) copy-start(pred[256]{0:T(512)(128)(4,1)} %constant.631) | copy-start | bytes 772
  0.0 28.4 %copy-start.9 = (pred[256]{0:T(512)(128)(4,1)S(1)}, pred[256]{0:T(512)(128)(4,1)}, u32[]{:S(2)}) copy-start(pred[256]{0:T(512)(128)(4,1)} %constant.630) | copy-start | bytes 772
  0.0 28.4 %copy-start.6 = (s32[256]{0:T(256)S(1)}, s32[256]{0:T(256)}, u32[]{:S(2)}) copy-start(s32[256]{0:T(256)} %constant.629) | copy-start | bytes 3076
  0.0 30.6 %copy-start = (bf16[64,128,128]{2,1,0:T(8,128)(2,1)S(1)}, bf16[64,128,128]{2,1,0:T(8,128)(2,1)}, u32[]{:S(2)}) copy-start(bf16[64,128,128]{2,1,0:T(8,128)(2,1)} %refs_0_) | copy-start | bytes 6291460
  13.3 17.4 %collective-permute-start.3 = (bf16[64,128,128]{2,1,0:T(8,128)(2,1)}, bf16[64,128,128]{2,1,0:T(8,128)(2,1)}, u32[]{:S(2)}, u32[]{:S(2)}) collective-permute-start(bf16[64,128,128]{2,1,0:T(8,128)(2,1)} %refs_0_), channel_id=1, source_target_pairs={{0,1},{1,0},{2,3},{3,2},{4,5},{5,4},{6,7},{7,6},{8,9},{9,8},{10,11... | collective-permute-start | bytes 6291464 | tf_op jit(solution)/shard_map/ppermute | solution.py:522
  15.3 89.4 %collective-permute-start.4 = (bf16[16,128,128]{2,1,0:T(8,128)(2,1)}, bf16[16,128,128]{2,1,0:T(8,128)(2,1)}, u32[]{:S(2)}, u32[]{:S(2)}) collective-permute-start(bf16[16,128,128]{2,1,0:T(8,128)(2,1)} %slice.89), channel_id=1, source_target_pairs={{0,16},{1,17},{2,18},{3,19},{4,20},{5,21},{6,22},{7,23},{8,24},{9,... | collective-permute-start | bytes 1572872 | tf_op jit(solution)/shard_map/ppermute | solution.py:521
  35.5 69.3 %collective-permute-start.5 = (bf16[38,128,128]{2,1,0:T(8,128)(2,1)}, bf16[38,128,128]{2,1,0:T(8,128)(2,1)S(1)}, u32[]{:S(2)}, u32[]{:S(2)}) collective-permute-start(bf16[38,128,128]{2,1,0:T(8,128)(2,1)} %get-tuple-element.153), channel_id=1, source_target_pairs={{0,16},{1,17},{2,18},{3,19},{4,20},{5,21},{6,22},{7,23},{8,24},{9,... | collective-permute-start | bytes 3735560 | tf_op jit(solution)/shard_map/ppermute | solution.py:527
  104.8 4.7 %copy-start.1 = (bf16[38,128,128]{2,1,0:T(8,128)(2,1)}, bf16[38,128,128]{2,1,0:T(8,128)(2,1)S(1)}, u32[]{:S(2)}) copy-start(bf16[38,128,128]{2,1,0:T(8,128)(2,1)S(1)} %collective-permute-done.5.refs_5_.refs_4_) | copy-start | bytes 3735556
  104.8 4.7 %collective-permute-start.7 = (bf16[38,128,128]{2,1,0:T(8,128)(2,1)S(1)}, bf16[38,128,128]{2,1,0:T(8,128)(2,1)}, u32[]{:S(2)}, u32[]{:S(2)}) collective-permute-start(bf16[38,128,128]{2,1,0:T(8,128)(2,1)S(1)} %collective-permute-done.5.refs_5_.refs_4_), channel_id=1, source_target_pairs={{0,1},{1,0},{2,3},{3,2},{4,5},{5,4},{6,7},{7,6},{8,9},{9,8},{10,11... | collective-permute-start | bytes 3735560 | tf_op jit(solution)/shard_map/ppermute | solution.py:531
  105.6 4.0 %collective-permute-start.6 = (bf16[16,128,128]{2,1,0:T(8,128)(2,1)}, bf16[16,128,128]{2,1,0:T(8,128)(2,1)}, u32[]{:S(2)}, u32[]{:S(2)}) collective-permute-start(bf16[16,128,128]{2,1,0:T(8,128)(2,1)} %collective-permute-done.4.refs_3_.refs_2_), channel_id=1, source_target_pairs={{0,1},{1,0},{2,3},{3,2},{4,5},{5,4},{6,7},{7,6},{8,9},{9,8},{10,11... | collective-permute-start | bytes 1572872 | tf_op jit(solution)/shard_map/ppermute | solution.py:530
  115.3 47.5 %copy-start.2 = (s32[64]{0:T(128)S(1)}, s32[64]{0:T(128)}, u32[]{:S(2)}) copy-start(s32[64]{0:T(128)} %read_ref.1) | copy-start | bytes 772

commit v3 on v2

--- a/solution.py
+++ b/solution.py
@@ -12,7 +12,7 @@
 CORES = 2
 HALVES = 2
 FAMILY = CORES * HALVES
-AHEAD = 2
+AHEAD = 4
 TOGETHER = 4
 
 
@@ -120,9 +120,9 @@
 
 def lane_sizes(blocks, devices):
     share = max(1, CORES * blocks * CORES // devices)
-    early, late = CORES * ((5 * share + 3) // 4), CORES * ((7 * share + 3) // 4)
+    early, late = CORES * ((9 * share + 7) // 8), CORES * ((7 * share + 3) // 4)
     kept = blocks // 4
-    cross = 4 * (CORES * (blocks - kept) // 5)
+    cross = 37 * (CORES * (blocks - kept)) // 48
     return early, late, kept, cross - cross % CORES
 
 
@@ -161,18 +161,25 @@
     return (load > late) | (crossing > cross)
 
 
-def plan(table, blocks, early, late, kept, cross):
+def orders_of(blocks, kept):
     devices = lax.axis_size("dev")
     families = devices // FAMILY
-    many = FAMILY * blocks
-    pair = CORES * blocks
     me = lax.axis_index("dev")
     half, family, core = me // (devices // HALVES), me // CORES % families, me % CORES
-    part = np.repeat(np.arange(HALVES), pair)
+    part = np.repeat(np.arange(HALVES), CORES * blocks)
     x_core = np.tile(np.repeat(np.arange(CORES), blocks), HALVES)
     x_block = np.tile(np.arange(blocks), FAMILY)
     order = np.lexsort((x_block, x_core, (part == 1) & (x_block >= kept), part))
     part, x_core, x_block = (jnp.asarray(v[order], jnp.int32) for v in (part, x_core, x_block))
+    return half, family, core, part, x_core, x_block
+
+
+def plan(table, blocks, early, late, kept, cross):
+    devices = lax.axis_size("dev")
+    families = devices // FAMILY
+    many = FAMILY * blocks
+    pair = CORES * blocks
+    half, family, core, part, x_core, x_block = orders_of(blocks, kept)
     x_half = jnp.where(half == 0, part, 1 - part)
     away = jnp.where(core == 0, x_core, 1 - x_core)
 
@@ -184,8 +191,9 @@
         [jnp.sum(jnp.where(inside, table[j][None], 0), axis=1) for j in range(CAP)]
     )
     chip = jnp.where(partners > 0, (partners - 1) // pair, -1)
-    f = iota(1, families, axis=1)
-    need = jnp.any(chip[:, :, None] == (f + half * families)[None], axis=0) & (f != family)
+    mask = iota(1, families, axis=1)
+    target = (family ^ mask) + half * families
+    need = jnp.any(chip[:, :, None] == target[None], axis=0) & (mask > 0)
     crosses = jnp.any((partners > 0) & (chip // families != x_half[None]), axis=0)
     crosses = crosses & (x_block >= kept)
     leaves, comes = crosses & (part == 0), crosses & (part == 1)
@@ -207,40 +215,55 @@
     spots = iota(1, side, 1, axis=1)[0] + core * side
     cross_send = jnp.sum(jnp.where(leaving[None] == spots, local[None], 0), axis=1)
 
-    def send(first, stop, lane):
+    def send(first, lane):
         spot = first[:, None, None] + iota(1, lane // CORES, 1, axis=1) + core * (lane // CORES)
-        hit = (rank[:, None, :] == spot) & (rank[:, None, :] < stop[:, None, None])
+        hit = (rank[:, None, :] == spot) & (part == 0)
         return jnp.sum(jnp.where(hit, local[None, None, :], 0), axis=2).reshape(-1)
 
     zero = jnp.zeros((families,), jnp.int32)
+    return cross_send, send(zero, early), (partners, rank, need, local)
+
+
+def late_plan(known, blocks, early, late, kept, cross):
+    partners, rank, need, local = known
+    devices = lax.axis_size("dev")
+    families = devices // FAMILY
+    many = FAMILY * blocks
+    pair = CORES * blocks
+    half, family, core, part, x_core, x_block = orders_of(blocks, kept)
+    x_half = jnp.where(half == 0, part, 1 - part)
     near_count = jnp.sum(i32(need & (part == 0)[:, None]), axis=0)
     shipped = jnp.minimum(near_count, early)
-    sends = send(zero, shipped, early), send(shipped, zero + many, late)
-
+    side = late // CORES
+    spot = shipped[:, None, None] + iota(1, side, 1, axis=1) + core * side
+    hit = rank[:, None, :] == spot
+    then = jnp.sum(jnp.where(hit, local[None, None, :], 0), axis=2).reshape(-1)
+
+    mask = iota(families, 1, axis=0)
     pairs = partners[:, :pair].reshape(-1)
     all_ids = (
-        ((x_half[None] * families + iota(families, 1, axis=0)) * CORES + x_core[None]) * blocks
+        ((x_half[None] * families + (family ^ mask)) * CORES + x_core[None]) * blocks
         + x_block[None]
         + 1
     ).reshape(1, -1)
     wanted = jnp.any(pairs[:, None] == all_ids, axis=0).reshape(families, many)
+    before = (iota(many, many, axis=0) < iota(many, many, axis=1)).astype(jnp.bfloat16)
     arrived = i32(
-        jnp.dot(wanted.astype(jnp.bfloat16), before.T, preferred_element_type=jnp.float32)
+        jnp.dot(wanted.astype(jnp.bfloat16), before, preferred_element_type=jnp.float32)
     )
     came = jnp.sum(i32(wanted & (part == 0)[None]), axis=1, keepdims=True)
     came = jnp.minimum(came, early)
     base = pair + CORES * kept + cross
-    g = iota(families, many, axis=0)
     place = jnp.where(
         arrived < came,
-        base + g * early + arrived,
-        base + families * early + g * late + arrived - came,
-    )
-    place = jnp.where(g == family, local[None], place).reshape(1, -1)
+        base + mask * early + arrived,
+        base + families * early + mask * late + arrived - came,
+    )
+    place = jnp.where(mask == 0, local[None], place).reshape(1, -1)
     empty = base + families * (early + late)
     own = lax.dynamic_slice(partners, (0, core * blocks), (CAP, blocks)).reshape(-1)
-    found = jnp.sum(jnp.where(own[:, None] == all_ids, place, 0), axis=1)
-    return cross_send, sends, jnp.where(own > 0, found, empty)
+    picked = jnp.sum(jnp.where(own[:, None] == all_ids, place, 0), axis=1)
+    return then, jnp.where(own > 0, picked, empty)
 
 
 def fill(refs, held, sems):
@@ -254,18 +277,19 @@
     return copies
 
 
-def pack_kernel(parts, *refs):
-    sends, near = refs[:parts], refs[parts : -2 - parts]
-    outs, (held, sems) = refs[-2 - parts : -2], refs[-2:]
+def pack_kernel(parts, send_ref, *refs):
+    near, outs, (held, sems) = refs[: -2 - parts], refs[-2 - parts : -2], refs[-2:]
     for copy in fill(near, held, sems):
         copy.wait()
-    for send_ref, out_ref in zip(sends, outs):
+    begin = 0
+    for out_ref in outs:
 
         def step(i, _):
-            out_ref[i] = held[send_ref[i]]
+            out_ref[i] = held[send_ref[begin + i]]
             return 0
 
         lax.fori_loop(0, out_ref.shape[0], step, 0, unroll=2)
+        begin += out_ref.shape[0]
 
 
 def tile_kernel(pick_ref, read_ref, *refs):
@@ -300,23 +324,22 @@
 VMEM = pl.BlockSpec(memory_space=pltpu.VMEM)
 
 
-def pack(sends, near):
+def pack(send, near, lanes=None):
     rows, kmers = near[0].shape[1:]
     total = sum(ref.shape[0] for ref in near)
+    lanes = lanes or [send.shape[0]]
     return pl.pallas_call(
-        functools.partial(pack_kernel, len(sends)),
-        out_shape=[
-            jax.ShapeDtypeStruct((send.shape[0], rows, kmers), near[0].dtype) for send in sends
-        ],
-        in_specs=[SMEM] * len(sends) + [HBM] * len(near),
-        out_specs=[VMEM] * len(sends),
+        functools.partial(pack_kernel, len(lanes)),
+        out_shape=[jax.ShapeDtypeStruct((lane, rows, kmers), near[0].dtype) for lane in lanes],
+        in_specs=[SMEM] + [HBM] * len(near),
+        out_specs=[VMEM] * len(lanes),
         scratch_shapes=[
             pltpu.VMEM((total, rows, kmers), near[0].dtype),
             pltpu.SemaphoreType.DMA((len(near),)),
         ],
         compiler_params=pltpu.CompilerParams(vmem_limit_bytes=60 << 20),
         name="pack",
-    )(*sends, *near)
+    )(send, *near)
 
 
 def tiles(pick, read_block, near):
@@ -345,14 +368,19 @@
     pl.semaphore_wait(barrier, len(others))
 
 
-def everyone_kernel(devices, row_ref, out_ref, send_sems, recv_sems):
+def everyone_kernel(
+    devices, row_ref, mine_ref, owners_ref, orders_ref, sibling_ref, lead_ref, got, lead, *sems
+):
+    send_sems, recv_sems, move_sems = sems
     me = lax.axis_index("dev")
-    out_ref[me] = row_ref[...]
+    load = pltpu.make_async_copy(mine_ref.at[pl.ds(0, lead.shape[0])], lead, move_sems.at[0])
+    load.start()
+    got[me] = row_ref[...]
     greet([(me + k) % devices for k in range(1, devices)])
     copies = [
         pltpu.make_async_remote_copy(
             src_ref=row_ref,
-            dst_ref=out_ref.at[me],
+            dst_ref=got.at[me],
             send_sem=send_sems.at[k],
             recv_sem=recv_sems.at[k],
             device_id=((me + k) % devices,),
@@ -362,21 +390,51 @@
     ]
     for copy in copies:
         copy.start()
+    swap = pltpu.make_async_remote_copy(
+        src_ref=mine_ref,
+        dst_ref=sibling_ref,
+        send_sem=send_sems.at[0],
+        recv_sem=recv_sems.at[0],
+        device_id=(me + 1 - 2 * (me % CORES),),
+        device_id_type=pl.DeviceIdType.MESH,
+    )
+    swap.start()
+    load.wait()
+    store = pltpu.make_async_copy(lead, lead_ref, move_sems.at[1])
+    store.start()
     for copy in copies:
         copy.wait()
-
-
-def gather_rows(row):
-    devices = lax.axis_size("dev")
+    owners_ref[...] = got[:, 0, :]
+    orders_ref[...] = got[:, 1, :]
+    store.wait()
+    swap.wait()
+
+
+def gather_rows(row, mine, kept):
+    devices = lax.axis_size("dev")
+    slots = row.shape[1]
+    table = jax.ShapeDtypeStruct((devices, slots), row.dtype)
+    lead = (kept,) + mine.shape[1:]
     return pl.pallas_call(
         functools.partial(everyone_kernel, devices),
-        out_shape=jax.ShapeDtypeStruct((devices,) + row.shape, row.dtype),
-        in_specs=[VMEM],
-        out_specs=VMEM,
-        scratch_shapes=[pltpu.SemaphoreType.DMA((devices,))] * 2,
+        out_shape=[
+            table,
+            table,
+            jax.ShapeDtypeStruct(mine.shape, mine.dtype),
+            jax.ShapeDtypeStruct(lead, mine.dtype),
+        ],
+        in_specs=[VMEM, HBM],
+        out_specs=[VMEM, VMEM, HBM, HBM],
+        scratch_shapes=[
+            pltpu.VMEM((devices,) + row.shape, row.dtype),
+            pltpu.VMEM(lead, mine.dtype),
+            pltpu.SemaphoreType.DMA((devices,)),
+            pltpu.SemaphoreType.DMA((devices,)),
+            pltpu.SemaphoreType.DMA((2,)),
+        ],
         compiler_params=pltpu.CompilerParams(has_side_effects=True, collective_id=0),
         name="gather_rows",
-    )(row)
+    )(row, mine)
 
 
 def flipped(value, mask):
@@ -441,70 +499,197 @@
     )(out)
 
 
-def swap_kernel(families, lane, out_ref, got_ref, send_sems, recv_sems, pass_sems, take_sems):
+def trade_kernel(devices, early, late, cuts, *refs):
+    then_ref, mine_ref, sibling_ref, far_ref, cross_ref, out_ref = refs[:6]
+    got_ref, also_ref, far_twin_ref, own_ref, twin_ref, held, lanes = refs[6:13]
+    fill_sems, cross_sems, soon_sems, last_sems = refs[13:]
+    families = devices // FAMILY
     me = lax.axis_index("dev")
     chip, core = me // CORES, me % CORES
     spot = chip % families
-    side = lane // CORES
-
-    def copy_of(k):
-        to = flipped(spot, k)
+    twin, opposite = chip * CORES + 1 - core, (me + devices // HALVES) % devices
+    blocks, kept, side = mine_ref.shape[0], far_ref.shape[0], cross_ref.shape[0]
+    at = {"far": CORES * blocks, "far_twin": CORES * blocks + kept}
+    at["own"] = CORES * blocks + CORES * kept
+    at["twin"] = at["own"] + side
+
+    def part(name, begin, size):
+        return held.at[pl.ds(at[name] + begin, size)]
+
+    def remote(src, dst, send_sem, recv_sem, to):
         return pltpu.make_async_remote_copy(
-            src_ref=out_ref.at[pl.ds(to * side, side)],
-            dst_ref=got_ref.at[pl.ds(spot * lane + core * side, side)],
-            send_sem=send_sems.at[k],
-            recv_sem=recv_sems.at[k],
-            device_id=((chip - spot + to) * CORES + core,),
+            src_ref=src,
+            dst_ref=dst,
+            send_sem=send_sem,
+            recv_sem=recv_sem,
+            device_id=(to,),
             device_id_type=pl.DeviceIdType.MESH,
         )
 
-    def pass_of(k):
-        rows = got_ref.at[pl.ds(flipped(spot, k) * lane + core * side, side)]
-        return pltpu.make_async_remote_copy(
-            src_ref=rows,
-            dst_ref=rows,
-            send_sem=pass_sems.at[k],
-            recv_sem=take_sems.at[k],
-            device_id=(chip * CORES + 1 - core,),
-            device_id_type=pl.DeviceIdType.MESH,
+    fills = [
+        pltpu.make_async_copy(mine_ref, held.at[pl.ds(0, blocks)], fill_sems.at[0]),
+        pltpu.make_async_copy(sibling_ref, held.at[pl.ds(blocks, blocks)], fill_sems.at[1]),
+        pltpu.make_async_copy(far_ref, part("far", 0, kept), fill_sems.at[2]),
+    ]
+    for copy in fills:
+        copy.start()
+    chips = {k: (chip - spot + flipped(spot, k)) * CORES + core for k in range(1, families)}
+    greet(list(chips.values()) + [twin, opposite])
+
+    crossing, passing = [], []
+    for i, (begin, size) in enumerate(cuts):
+        here = part("own", begin, size)
+        crossing.append(
+            remote(
+                cross_ref.at[pl.ds(begin, size)],
+                here,
+                cross_sems.at[4 * i],
+                cross_sems.at[4 * i + 1],
+                opposite,
+            )
         )
-
-    chips = [(chip - spot + flipped(spot, k)) * CORES + core for k in range(1, families)]
-    greet(chips + [chip * CORES + 1 - core])
+        passing.append(
+            remote(
+                here,
+                part("twin", begin, size),
+                cross_sems.at[4 * i + 2],
+                cross_sems.at[4 * i + 3],
+                twin,
+            )
+        )
+    last = 4 * len(cuts)
+    share = remote(
+        far_ref, part("far_twin", 0, kept), cross_sems.at[last], cross_sems.at[last + 1], twin
+    )
+    for copy in crossing:
+        copy.start()
+    share.start()
+
     top = families - 1
     steps = [[k for k in (m, top - m) if k] for m in range(top, families // 2 - 1, -1)]
-    copies = [[copy_of(k) for k in step] for step in steps]
-    passes = [[pass_of(k) for k in step] for step in steps]
-    for i in range(len(steps) + AHEAD):
-        if i >= AHEAD:
-            for copy in copies[i - AHEAD]:
-                copy.wait_send()
-        if i < len(steps):
-            for copy in copies[i]:
-                copy.start()
-        if i >= AHEAD:
-            for copy, follow in zip(copies[i - AHEAD], passes[i - AHEAD]):
-                copy.wait_recv()
-                follow.start()
-    for step in passes:
+
+    def lanes_of(src_ref, dst_ref, lane, sems):
+        size = lane // CORES
+        sent, passed = [], []
+        for step in steps:
+            sent.append([])
+            passed.append([])
+            for k in step:
+                begin = k * lane + core * size
+                rows = dst_ref.at[pl.ds(begin, size)]
+                src = src_ref.at[pl.ds(k * size, size)]
+                sent[-1].append(remote(src, rows, sems.at[4 * k], sems.at[4 * k + 1], chips[k]))
+                passed[-1].append(
+                    remote(rows, rows, sems.at[4 * k + 2], sems.at[4 * k + 3], twin)
+                )
+        return sent, passed
+
+    def start(sent, i):
+        for copy in sent[i]:
+            copy.start()
+
+    def finish(sent, i):
+        for copy in sent[i]:
+            copy.wait_send()
+
+    def land(sent, passed, i):
+        for copy, follow in zip(sent[i], passed[i]):
+            copy.wait_recv()
+            follow.start()
+
+    count = len(steps)
+    ahead = min(AHEAD, count)
+    soon, soon_passed = lanes_of(out_ref, got_ref, early, soon_sems)
+    for i in range(count):
+        if i >= ahead:
+            finish(soon, i - ahead)
+        start(soon, i)
+        if i >= ahead:
+            land(soon, soon_passed, i - ahead)
+
+    for copy, follow in zip(crossing, passing):
+        copy.wait_recv()
+        follow.start()
+    for copy in fills:
+        copy.wait()
+    share.wait_recv()
+    for follow in passing:
+        follow.wait_recv()
+    stores = [
+        pltpu.make_async_copy(part("far_twin", 0, kept), far_twin_ref, fill_sems.at[3]),
+        pltpu.make_async_copy(part("own", 0, side), own_ref, fill_sems.at[4]),
+        pltpu.make_async_copy(part("twin", 0, side), twin_ref, fill_sems.at[5]),
+    ]
+    for copy in stores:
+        copy.start()
+
+    size = late // CORES
+    for step in steps:
+        for k in step:
+
+            def move(i, _):
+                lanes[k * size + i] = held[then_ref[k * size + i]]
+                return 0
+
+            lax.fori_loop(0, size, move, 0, unroll=2)
+
+    late_sent, late_passed = lanes_of(lanes, also_ref, late, last_sems)
+    for i in range(ahead):
+        start(late_sent, i)
+    for i in range(count - ahead, count):
+        finish(soon, i)
+        land(soon, soon_passed, i)
+    for i in range(ahead, count):
+        finish(late_sent, i - ahead)
+        start(late_sent, i)
+        land(late_sent, late_passed, i - ahead)
+    for i in range(count - ahead, count):
+        finish(late_sent, i)
+        land(late_sent, late_passed, i)
+    for copy in crossing + passing + [share]:
+        copy.wait_send()
+    for copy in stores:
+        copy.wait()
+    for step in soon_passed + late_passed:
         for follow in step:
             follow.wait()
 
 
-def swap_lanes(out, lane, number):
-    families = lax.axis_size("dev") // FAMILY
+def trade(then, mine, sibling, far, crossing, out, early, late):
+    devices = lax.axis_size("dev")
+    families = devices // FAMILY
+    shape, kind = mine.shape[1:], mine.dtype
+    kept, side = far.shape[0], crossing.shape[0]
+    cuts = [(0, side // 2), (side // 2, side - side // 2)]
+    held = CORES * (mine.shape[0] + kept + side)
+
+    def rows(count):
+        return jax.ShapeDtypeStruct((count,) + shape, kind)
+
     return pl.pallas_call(
-        functools.partial(swap_kernel, families, lane),
-        out_shape=jax.ShapeDtypeStruct((families * lane,) + out.shape[1:], out.dtype),
-        in_specs=[HBM],
-        out_specs=HBM,
-        scratch_shapes=[pltpu.SemaphoreType.DMA((families,))] * 4,
-        compiler_params=pltpu.CompilerParams(has_side_effects=True, collective_id=number),
-        cost_estimate=pl.CostEstimate(
-            flops=0, bytes_accessed=32 * out.size * out.dtype.itemsize, transcendentals=0
+        functools.partial(trade_kernel, devices, early, late, cuts),
+        out_shape=[
+            rows(families * early),
+            rows(families * late),
+            rows(kept),
+            rows(side),
+            rows(side),
+        ],
+        in_specs=[SMEM] + [HBM] * 5,
+        out_specs=[HBM] * 5,
+        scratch_shapes=[
+            pltpu.VMEM((held,) + shape, kind),
+            pltpu.VMEM((families * late // CORES,) + shape, kind),
+            pltpu.SemaphoreType.DMA((6,)),
+            pltpu.SemaphoreType.DMA((4 * len(cuts) + 2,)),
+            pltpu.SemaphoreType.DMA((4 * families,)),
+            pltpu.SemaphoreType.DMA((4 * families,)),
+        ],
+        compiler_params=pltpu.CompilerParams(
+            has_side_effects=True, collective_id=1, vmem_limit_bytes=60 << 20
         ),
-        name="swap_lanes",
-    )(out)
+        name="trade",
+    )(then, mine, sibling, far, crossing, out)
 
 
 def shards(occurrence, block_owner, read_block, slot_order):
@@ -516,31 +701,29 @@
     swap = [(d, d ^ 1) for d in range(devices)]
     across = [(d, (d + devices // HALVES) % devices) for d in range(devices)]
     row = jnp.stack([jnp.pad(block_owner[:, 0], (0, slots - blocks)), slot_order[0]])
-    everyone = gather_rows(row)
-    everyone, mine = lax.optimization_barrier((everyone, occurrence))
-    far = lax.ppermute(mine[:kept], "dev", across)
-    sibling = lax.ppermute(mine, "dev", swap)
-    table = group_table(everyone[:, 0, :blocks], everyone[:, 1])
-    cross_send, sends, pick = plan(table, blocks, early, late, kept, cross)
-    full = too_full(table, blocks, early, late, kept, cross)
-    crossing, out = pack((cross_send, sends[0]), (mine, sibling))
-    crossed = lax.ppermute(crossing, "dev", across)
-    got = swap_lanes(out, early, 1)
-    far, crossed, got = lax.optimization_barrier((far, crossed, got))
-    near = (mine, sibling, far, lax.ppermute(far, "dev", swap))
-    near = near + (crossed, lax.ppermute(crossed, "dev", swap))
-    also = swap_lanes(pack((sends[1],), near)[0], late, 2)
-    first = tiles(pick, read_block, near + (got, also))
+    mine = occurrence
+    owners, orders, sibling, lead = gather_rows(row, mine, kept)
+    far = lax.ppermute(lead, "dev", across)
+    table = group_table(owners[:, :blocks], orders)
+    sizes = blocks, early, late, kept, cross
+    cross_send, send, known = plan(table, *sizes)
+    lanes = cross // CORES, send.shape[0]
+    crossing, out = pack(jnp.concatenate([cross_send, send]), (mine, sibling), lanes)
+    then, pick = late_plan(known, *sizes)
+    full = too_full(table, *sizes)
+    far, then, pick, full = lax.optimization_barrier((far, then, pick, full))
+    got, also, far_twin, own, twin = trade(then, mine, sibling, far, crossing, out, early, late)
+    first = tiles(pick, read_block, (mine, sibling, far, far_twin, own, twin, got, also))
 
     def more(carry):
-        begin, stop, margin = carry
+        begin, _, margin = carry
         begin, now, mine = lax.optimization_barrier((begin, table, occurrence))
         send, pick, local = routes(now, blocks)
         sibling = lax.ppermute(mine, "dev", swap)
         far = lax.ppermute(mine, "dev", across)
         near = (mine, sibling, far, lax.ppermute(far, "dev", swap))
-        got = exchange(pack((send(begin, spill, False),), near[:CORES])[0], spill)
-        also = exchange(pack((send(begin, spill, True),), near[CORES:])[0], spill)
+        got = exchange(pack(send(begin, spill, False), near[:CORES])[0], spill)
+        also = exchange(pack(send(begin, spill, True), near[CORES:])[0], spill)
         added = tiles(pick(begin, spill, local), read_block, near + (got, also))
         margin = jnp.where(begin == 0, 0.0, margin) + added
         return begin + CORES * spill, i32(fullest_lane(now, blocks)), margin

time: 176 us -> 160 us (0.909)
  Pallas kernels: 149 us -> 134 us
  waiting for transfers between devices: 0.01 us -> 4.18 us
  starting transfers between devices: 3.79 us -> 0.65 us
  local copies, waits for them, and re-layouts: 6.85 us -> 4.21 us
    pallas_call x5 -> x3, Pallas kernels: 137 us -> 121 us  [the longest x1 104 us: trade(): pl.pallas_call(functools.partial(trade_kernel, devices, early, late, cuts...]
    ppermute x5 -> x1, waiting for transfers between devices: 0.01 us -> 4.18 us  [shards(): far = lax.ppermute(lead, 'dev', across)]
    slice x4 -> x0, local copies, waits for them, and re-layouts: 3.57 us -> none  [the longest x1 1.91 us: shards(): far = lax.ppermute(mine[:kept], 'dev', across)]
    ppermute x5 -> x1, starting transfers between devices: 3.79 us -> 0.65 us  [shards(): far = lax.ppermute(lead, 'dev', across)]
  transfers between devices with their start and end apart: 5 -> 1, of which waited for: 0 -> 1; matrix products, arithmetic and copies ran while one was open for 11% -> 10% of each run, Pallas kernels for 41% -> 3%
where the time goes in v3:
time: 160 us; the launch traced here: 159 us
  Pallas kernels  134 us (84%)
  other arithmetic  12.9 us (8%)
  local copies, waits for them, and re-layouts  4.21 us (3%)
  waiting for transfers between devices  4.18 us (3%)
  between operations  1.79 us (1%)
    pallas_call x1, Pallas kernels, trade(): pl.pallas_call(functools.partial(trade_kernel, devices, early, late, cuts...  104 us
    pallas_call x1, Pallas kernels, gather_rows(): pl.pallas_call(functools.partial(everyone_kernel, devices), out_shape=[ta...  13.2 us
    pallas_call x1, Pallas kernels, tiles(): pl.pallas_call(tile_kernel, out_shape=jax.ShapeDtypeStruct((RB_DEV * rows...  12.5 us
    pallas_call x1, Pallas kernels, pack(): pl.pallas_call(functools.partial(pack_kernel, len(lanes)), out_shape=[jax...  4.73 us
    ppermute x1, waiting for transfers between devices, shards(): far = lax.ppermute(lead, 'dev', across)  4.18 us
  transfers between devices with their start and end apart: 1, of which 1 were waited for; matrix products, arithmetic and copies ran while one was open for 10% of the time, Pallas kernels for 3%

profile of v3, /device:TPU:0, one launch (start us, length us, event | category | flops | bytes accessed | tf_op | source)
XLA Modules:
  0.0 159.1 jit_solution(7510159651316414038)
XLA Ops:
  0.1 0.7 pad_bitcast_fusion
  0.8 1.2 pad_add_fusion.2.row_ref
  2.0 13.2 %gather_rows.1 = (s32[32,128]{1,0:T(8,128)}, s32[32,128]{1,0:T(8,128)}, bf16[64,128,128]{2,1,0:T(8,128)(2,1)}, bf16[16,128,128]{2,1,0:T(8,128)(2,1)}) custom-call(s32[2,128]{1,0:T(2,128)} %pad_add_fusion.2.row_ref, bf16[64,128,128]{2,1,0:T(8,128)(2,1)} %refs_0_.3), custom_call_target="tpu_custom_call" | custom-call | tf_op jit(solution)/shard_map/gather_rows/pallas_call | solution.py:418
  15.2 0.6 collective-permute-start.3
  15.9 1.7 %convert_reduce_fusion.1 = s32[32,64]{1,0:T(8,128)S(1)} fusion(s32[32,64]{1,0:T(8,128)} %bitcast.87, pred[64,64]{1,0:T(8,128)(4,1)S(1)} %iota_compare_fusion.10), kind=kLoop, calls=%fused_computation.144 | loop fusion | flops 522240 | bytes 20480 | tf_op jit(solution)/shard_map/reduce_sum | solution.py:33
  17.6 0.7 multiply_add_fusion
  18.4 0.1 add_add_fusion.2
  18.4 0.7 select_reduce_fusion.12
  19.1 0.1 copy.24
  19.2 0.1 copy.25
  19.3 0.1 copy.26
  19.4 0.8 copy.22
  20.2 0.1 copy.23
  20.3 2.9 %select_reduce_fusion.7 = s32[4,32,32]{2,1,0:T(8,128)S(1)} fusion(s32[32,128]{1,0:T(8,128)S(1)} %copy.26, s32[4,32,32]{2,1,0:T(8,128)S(1)} %copy.23), kind=kLoop, calls=%fused_computation.131 | loop fusion | flops 1568768 | bytes 49152 | tf_op jit(solution)/shard_map/reduce_sum | solution.py:41
  23.2 0.1 eq.524
  23.3 0.1 eq.529
  23.4 0.1 eq.532
  23.5 0.1 eq.535
  23.6 0.9 select_reduce_fusion.11
  24.6 0.1 compare_reduce_fusion.3
  24.7 0.2 convert_reduce_fusion.5
  24.9 0.2 fusion.50
  25.1 0.1 reshape.673
  25.4 0.3 select_reduce_fusion.14
  25.7 0.1 copy.28
  25.8 0.1 reshape.674
  25.9 0.1 constant_dynamic-slice_fusion.1
  26.0 0.1 add_bitcast_fusion
  26.0 0.7 compare_reduce_fusion.2
  26.7 0.1 convert_reduce_fusion.4
  26.9 0.4 select_reduce_fusion.13
  27.4 0.1 fusion.67
  27.5 0.2 select_reduce_fusion.15
  27.7 0.1 select_bitcast_fusion
  27.8 0.8 fusion.66
  28.6 0.6 pad_add_fusion.3.send_ref
  29.2 0.1 reshape.671
  29.3 0.1 copy.27
  29.4 0.6 reshape.670.refs_0_
  30.0 4.7 %pack.3 = (bf16[37,128,128]{2,1,0:T(8,128)(2,1)}, bf16[72,128,128]{2,1,0:T(8,128)(2,1)}) custom-call(s32[109]{0:T(128)} %pad_add_fusion.3.send_ref, bf16[64,128,128]{2,1,0:T(8,128)(2,1)S(1)} %copy-done, bf16[64,128,128]{2,1,0:T(8,128)(2,1)} %get-tuple-element.164.refs_1_.refs_2_), custom_call_target="tpu_custom_call" | custom-call | tf_op jit(solution)/shard_map/pack/pallas_call | solution.py:331
  35.3 0.8 fusion.51
  36.7 0.3 select_reduce_fusion.6
  37.0 0.6 compare_select_fusion.11.pick_ref
  37.6 4.2 %collective-permute-done.3.refs_3_.refs_2_ = bf16[16,128,128]{2,1,0:T(8,128)(2,1)S(1)} collective-permute-done((bf16[16,128,128]{2,1,0:T(8,128)(2,1)}, bf16[16,128,128]{2,1,0:T(8,128)(2,1)S(1)}, u32[]{:S(2)}, u32[]{:S(2)}) %collective-permute-start.3) | collective-permute-done | bytes 524320 | tf_op jit(solution)/shard_map/ppermute | solution.py:706
  41.8 0.8 copy-done.1
  42.6 103.6 %trade.1 = (bf16[144,128,128]{2,1,0:T(8,128)(2,1)}, bf16[224,128,128]{2,1,0:T(8,128)(2,1)}, bf16[16,128,128]{2,1,0:T(8,128)(2,1)}, bf16[37,128,128]{2,1,0:T(8,128)(2,1)}, bf16[37,128,128]{2,1,0:T(8,128)(2,1)}) custom-call(s32[112]{0:T(128)} %reshape.670.refs_0_, bf16[64,128,128]{2,1,0:T(8,128)(2,1)S(1)} %copy-done, ...), custom_call_target="tpu_custom_call" | custom-call | tf_op jit(solution)/shard_map/trade/pallas_call | solution.py:669
  146.2 12.5 %tiles.6 = f32[2048,512]{1,0:T(8,128)} custom-call(s32[256]{0:T(256)} %compare_select_fusion.11.pick_ref, s32[64]{0:T(128)S(1)} %copy-done.2, bf16[64,128,128]{2,1,0:T(8,128)(2,1)S(1)} %copy-done, bf16[64,128,128]{2,1,0:T(8,128)(2,1)} %get-tuple-element.164.refs_1_.refs_2_, bf16[16,128,128]{2,1,0:T(8,128)(2,1)} %copy-done.1, ...), custom_call_target="tpu_custom_call" | custom-call | tf_op jit(solution)/shard_map/tiles/pallas_call | solution.py:348
  158.8 0.2 while.15
  (56 shorter events, 0.4 us)
Async XLA Ops:
  0.0 23.5 %copy-start.7 = (s32[256]{0:T(256)S(1)}, s32[256]{0:T(256)}, u32[]{:S(2)}) copy-start(s32[256]{0:T(256)} %constant.627.clone) | copy-start | bytes 3076
  0.0 23.5 %copy-start.4 = (s32[256]{0:T(256)S(1)}, s32[256]{0:T(256)}, u32[]{:S(2)}) copy-start(s32[256]{0:T(256)} %constant.628.clone) | copy-start | bytes 3076
  0.0 23.5 %copy-start.5 = (s32[256]{0:T(256)S(1)}, s32[256]{0:T(256)}, u32[]{:S(2)}) copy-start(s32[256]{0:T(256)} %constant.629.clone) | copy-start | bytes 3076
  0.0 23.5 %copy-start.8 = (s32[256]{0:T(256)S(1)}, s32[256]{0:T(256)}, u32[]{:S(2)}) copy-start(s32[256]{0:T(256)} %constant.634) | copy-start | bytes 3076
  0.0 24.5 %copy-start.3 = (pred[256]{0:T(512)(128)(4,1)S(1)}, pred[256]{0:T(512)(128)(4,1)}, u32[]{:S(2)}) copy-start(pred[256]{0:T(512)(128)(4,1)} %constant.636) | copy-start | bytes 772
  0.0 24.5 %copy-start.9 = (pred[256]{0:T(512)(128)(4,1)S(1)}, pred[256]{0:T(512)(128)(4,1)}, u32[]{:S(2)}) copy-start(pred[256]{0:T(512)(128)(4,1)} %constant.635) | copy-start | bytes 772
  0.0 24.5 %copy-start.10 = (pred[256]{0:T(512)(128)(4,1)S(1)}, pred[256]{0:T(512)(128)(4,1)}, u32[]{:S(2)}) copy-start(pred[256]{0:T(512)(128)(4,1)} %constant.637) | copy-start | bytes 772
  0.0 25.3 %copy-start.6 = (s32[256]{0:T(256)S(1)}, s32[256]{0:T(256)}, u32[]{:S(2)}) copy-start(s32[256]{0:T(256)} %constant.639) | copy-start | bytes 3076
  0.1 25.3 %copy-start.11 = (pred[256]{0:T(512)(128)(4,1)S(1)}, pred[256]{0:T(512)(128)(4,1)}, u32[]{:S(2)}) copy-start(pred[256]{0:T(512)(128)(4,1)} %constant.640) | copy-start | bytes 772
  2.0 27.9 %copy-start = (bf16[64,128,128]{2,1,0:T(8,128)(2,1)S(1)}, bf16[64,128,128]{2,1,0:T(8,128)(2,1)}, u32[]{:S(2)}) copy-start(bf16[64,128,128]{2,1,0:T(8,128)(2,1)} %refs_0_.3) | copy-start | bytes 6291460
  15.2 26.6 %collective-permute-start.3 = (bf16[16,128,128]{2,1,0:T(8,128)(2,1)}, bf16[16,128,128]{2,1,0:T(8,128)(2,1)S(1)}, u32[]{:S(2)}, u32[]{:S(2)}) collective-permute-start(bf16[16,128,128]{2,1,0:T(8,128)(2,1)} %get-tuple-element.159), channel_id=1, source_target_pairs={{0,16},{1,17},{2,18},{3,19},{4,20},{5,21},{6,22},{7,23},{8,24},{9,... | collective-permute-start | bytes 1572872 | tf_op jit(solution)/shard_map/ppermute | solution.py:706
  41.8 0.8 copy-start.1
  42.6 103.6 %copy-start.2 = (s32[64]{0:T(128)S(1)}, s32[64]{0:T(128)}, u32[]{:S(2)}) copy-start(s32[64]{0:T(128)} %read_ref.1) | copy-start | bytes 772

commit v4 on v3

--- a/solution.py
+++ b/solution.py
@@ -12,7 +12,7 @@
 CORES = 2
 HALVES = 2
 FAMILY = CORES * HALVES
-AHEAD = 4
+AHEAD = 4, 4
 TOGETHER = 4
 
 
@@ -120,7 +120,9 @@
 
 def lane_sizes(blocks, devices):
     share = max(1, CORES * blocks * CORES // devices)
-    early, late = CORES * ((9 * share + 7) // 8), CORES * ((7 * share + 3) // 4)
+    soon, rest = 2.1 * share, 1.26 * share
+    early = CORES * round((soon + 0.8 * soon**0.5) / CORES)
+    late = CORES * round((rest + 4.4 * rest**0.5) / CORES)
     kept = blocks // 4
     cross = 37 * (CORES * (blocks - kept)) // 48
     return early, late, kept, cross - cross % CORES
@@ -143,14 +145,18 @@
     families = devices // FAMILY
     held, packed = chip_counts(table, blocks, kept)
     here = (held > 0).astype(jnp.bfloat16)
-    demand = jnp.einsum(
-        "gc,gd->cd", held.astype(jnp.bfloat16), here, preferred_element_type=jnp.float32
-    )
+    both = jnp.concatenate([held, packed], axis=1).astype(jnp.bfloat16)
+    demand = jnp.einsum("gc,gd->cd", both, here, preferred_element_type=jnp.float32)
+    demand, last = demand[:chips], demand[chips:]
     c, d = iota(chips, chips, axis=0), iota(chips, chips, axis=1)
-    near = jnp.where(c // families == d // families, demand, 0.0)
-    far = jnp.where(c // families != d // families, demand, 0.0)
-    other = jnp.concatenate([far[families:], far[:families]], axis=0)
-    load = other + jnp.maximum(near - early, 0.0)
+    beyond = c // families != d // families
+
+    def turned(far):
+        return jnp.concatenate([far[families:], far[:families]], axis=0)
+
+    last = turned(jnp.where(beyond, last, 0.0))
+    soon = jnp.where(beyond, 0.0, demand) + turned(jnp.where(beyond, demand, 0.0)) - last
+    load = last + jnp.maximum(soon - early, 0.0)
     load = jnp.max(jnp.where(c % families != d % families, load, 0.0))
     halves = jnp.max(here.reshape(-1, HALVES, families), axis=2)
     crossing = jnp.einsum(
@@ -215,13 +221,7 @@
     spots = iota(1, side, 1, axis=1)[0] + core * side
     cross_send = jnp.sum(jnp.where(leaving[None] == spots, local[None], 0), axis=1)
 
-    def send(first, lane):
-        spot = first[:, None, None] + iota(1, lane // CORES, 1, axis=1) + core * (lane // CORES)
-        hit = (rank[:, None, :] == spot) & (part == 0)
-        return jnp.sum(jnp.where(hit, local[None, None, :], 0), axis=2).reshape(-1)
-
-    zero = jnp.zeros((families,), jnp.int32)
-    return cross_send, send(zero, early), (partners, rank, need, local)
+    return cross_send, (partners, rank, need, local)
 
 
 def late_plan(known, blocks, early, late, kept, cross):
@@ -232,13 +232,15 @@
     pair = CORES * blocks
     half, family, core, part, x_core, x_block = orders_of(blocks, kept)
     x_half = jnp.where(half == 0, part, 1 - part)
-    near_count = jnp.sum(i32(need & (part == 0)[:, None]), axis=0)
-    shipped = jnp.minimum(near_count, early)
-    side = late // CORES
-    spot = shipped[:, None, None] + iota(1, side, 1, axis=1) + core * side
-    hit = rank[:, None, :] == spot
-    then = jnp.sum(jnp.where(hit, local[None, None, :], 0), axis=2).reshape(-1)
-
+    soon = (part == 0) | (x_block < kept)
+    shipped = jnp.minimum(jnp.sum(i32(need & soon[:, None]), axis=0), early)
+
+    def send(first, allowed, side):
+        spot = first[:, None, None] + iota(1, side, 1, axis=1) + core * side
+        hit = (rank[:, None, :] == spot) & allowed
+        return jnp.sum(jnp.where(hit, local[None, None, :], 0), axis=2).reshape(-1)
+
+    sends = send(0 * shipped, soon[None, None, :], early // CORES), send(shipped, True, late // CORES)
     mask = iota(families, 1, axis=0)
     pairs = partners[:, :pair].reshape(-1)
     all_ids = (
@@ -251,7 +253,7 @@
     arrived = i32(
         jnp.dot(wanted.astype(jnp.bfloat16), before, preferred_element_type=jnp.float32)
     )
-    came = jnp.sum(i32(wanted & (part == 0)[None]), axis=1, keepdims=True)
+    came = jnp.sum(i32(wanted & soon[None]), axis=1, keepdims=True)
     came = jnp.minimum(came, early)
     base = pair + CORES * kept + cross
     place = jnp.where(
@@ -263,7 +265,7 @@
     empty = base + families * (early + late)
     own = lax.dynamic_slice(partners, (0, core * blocks), (CAP, blocks)).reshape(-1)
     picked = jnp.sum(jnp.where(own[:, None] == all_ids, place, 0), axis=1)
-    return then, jnp.where(own > 0, picked, empty)
+    return jnp.concatenate(sends), jnp.where(own > 0, picked, empty)
 
 
 def fill(refs, held, sems):
@@ -500,9 +502,9 @@
 
 
 def trade_kernel(devices, early, late, cuts, *refs):
-    then_ref, mine_ref, sibling_ref, far_ref, cross_ref, out_ref = refs[:6]
-    got_ref, also_ref, far_twin_ref, own_ref, twin_ref, held, lanes = refs[6:13]
-    fill_sems, cross_sems, soon_sems, last_sems = refs[13:]
+    send_ref, mine_ref, sibling_ref, far_ref, cross_ref = refs[:5]
+    got_ref, also_ref, far_twin_ref, own_ref, twin_ref, held, crossed, first, lanes = refs[5:14]
+    fill_sems, cross_sems, soon_sems, last_sems = refs[14:]
     families = devices // FAMILY
     me = lax.axis_index("dev")
     chip, core = me // CORES, me % CORES
@@ -510,11 +512,11 @@
     twin, opposite = chip * CORES + 1 - core, (me + devices // HALVES) % devices
     blocks, kept, side = mine_ref.shape[0], far_ref.shape[0], cross_ref.shape[0]
     at = {"far": CORES * blocks, "far_twin": CORES * blocks + kept}
-    at["own"] = CORES * blocks + CORES * kept
-    at["twin"] = at["own"] + side
 
     def part(name, begin, size):
-        return held.at[pl.ds(at[name] + begin, size)]
+        if name in at:
+            return held.at[pl.ds(at[name] + begin, size)]
+        return crossed.at[pl.ds(begin if name == "own" else side + begin, size)]
 
     def remote(src, dst, send_sem, recv_sem, to):
         return pltpu.make_async_remote_copy(
@@ -597,9 +599,31 @@
             copy.wait_recv()
             follow.start()
 
+    base = held.shape[0]
+
+    def block_of(at, everything):
+        if not everything:
+            return held[at]
+        near = held[jnp.minimum(at, base - 1)]
+        return jnp.where(at < base, near, crossed[jnp.maximum(at - base, 0)])
+
+    def gather(into, skip, size, everything):
+        for step in steps:
+            for k in step:
+
+                def move(i, _):
+                    into[k * size + i] = block_of(send_ref[skip + k * size + i], everything)
+                    return 0
+
+                lax.fori_loop(0, size, move, 0, unroll=2)
+
+    for copy in fills:
+        copy.wait()
+    share.wait_recv()
+    gather(first, 0, early // CORES, False)
     count = len(steps)
-    ahead = min(AHEAD, count)
-    soon, soon_passed = lanes_of(out_ref, got_ref, early, soon_sems)
+    ahead, behind = (min(most, count) for most in AHEAD)
+    soon, soon_passed = lanes_of(first, got_ref, early, soon_sems)
     for i in range(count):
         if i >= ahead:
             finish(soon, i - ahead)
@@ -610,9 +634,6 @@
     for copy, follow in zip(crossing, passing):
         copy.wait_recv()
         follow.start()
-    for copy in fills:
-        copy.wait()
-    share.wait_recv()
     for follow in passing:
         follow.wait_recv()
     stores = [
@@ -623,29 +644,19 @@
     for copy in stores:
         copy.start()
 
-    size = late // CORES
-    for step in steps:
-        for k in step:
-
-            def move(i, _):
-                lanes[k * size + i] = held[then_ref[k * size + i]]
-                return 0
-
-            lax.fori_loop(0, size, move, 0, unroll=2)
-
+    gather(lanes, families * (early // CORES), late // CORES, True)
     late_sent, late_passed = lanes_of(lanes, also_ref, late, last_sems)
-    for i in range(ahead):
-        start(late_sent, i)
-    for i in range(count - ahead, count):
-        finish(soon, i)
-        land(soon, soon_passed, i)
-    for i in range(ahead, count):
-        finish(late_sent, i - ahead)
-        start(late_sent, i)
-        land(late_sent, late_passed, i - ahead)
-    for i in range(count - ahead, count):
-        finish(late_sent, i)
-        land(late_sent, late_passed, i)
+    for i in range(count + behind):
+        if i >= behind:
+            finish(late_sent, i - behind)
+        if i < count:
+            start(late_sent, i)
+        if i == count - 1:
+            for j in range(count - ahead, count):
+                finish(soon, j)
+                land(soon, soon_passed, j)
+        if i >= behind:
+            land(late_sent, late_passed, i - behind)
     for copy in crossing + passing + [share]:
         copy.wait_send()
     for copy in stores:
@@ -655,13 +666,13 @@
             follow.wait()
 
 
-def trade(then, mine, sibling, far, crossing, out, early, late):
+def trade(send, mine, sibling, far, crossing, early, late):
     devices = lax.axis_size("dev")
     families = devices // FAMILY
     shape, kind = mine.shape[1:], mine.dtype
     kept, side = far.shape[0], crossing.shape[0]
     cuts = [(0, side // 2), (side // 2, side - side // 2)]
-    held = CORES * (mine.shape[0] + kept + side)
+    held = CORES * (mine.shape[0] + kept)
 
     def rows(count):
         return jax.ShapeDtypeStruct((count,) + shape, kind)
@@ -675,10 +686,12 @@
             rows(side),
             rows(side),
         ],
-        in_specs=[SMEM] + [HBM] * 5,
+        in_specs=[SMEM] + [HBM] * 4,
         out_specs=[HBM] * 5,
         scratch_shapes=[
             pltpu.VMEM((held,) + shape, kind),
+            pltpu.VMEM((CORES * side,) + shape, kind),
+            pltpu.VMEM((families * early // CORES,) + shape, kind),
             pltpu.VMEM((families * late // CORES,) + shape, kind),
             pltpu.SemaphoreType.DMA((6,)),
             pltpu.SemaphoreType.DMA((4 * len(cuts) + 2,)),
@@ -689,7 +702,7 @@
             has_side_effects=True, collective_id=1, vmem_limit_bytes=60 << 20
         ),
         name="trade",
-    )(then, mine, sibling, far, crossing, out)
+    )(send, mine, sibling, far, crossing)
 
 
 def shards(occurrence, block_owner, read_block, slot_order):
@@ -706,13 +719,12 @@
     far = lax.ppermute(lead, "dev", across)
     table = group_table(owners[:, :blocks], orders)
     sizes = blocks, early, late, kept, cross
-    cross_send, send, known = plan(table, *sizes)
-    lanes = cross // CORES, send.shape[0]
-    crossing, out = pack(jnp.concatenate([cross_send, send]), (mine, sibling), lanes)
-    then, pick = late_plan(known, *sizes)
+    cross_send, known = plan(table, *sizes)
+    crossing = pack(cross_send, (mine, sibling))[0]
+    send, pick = late_plan(known, *sizes)
     full = too_full(table, *sizes)
-    far, then, pick, full = lax.optimization_barrier((far, then, pick, full))
-    got, also, far_twin, own, twin = trade(then, mine, sibling, far, crossing, out, early, late)
+    far, send, pick, full = lax.optimization_barrier((far, send, pick, full))
+    got, also, far_twin, own, twin = trade(send, mine, sibling, far, crossing, early, late)
     first = tiles(pick, read_block, (mine, sibling, far, far_twin, own, twin, got, also))
 
     def more(carry):

time: 160 us -> 154 us (0.963)
  Pallas kernels: 134 us -> 127 us
    pallas_call x1, Pallas kernels: 104 us -> 98.1 us  [trade(): pl.pallas_call(functools.partial(trade_kernel, devices, early, late, cuts...]
  transfers between devices with their start and end apart: 1 -> 1, of which waited for: 1 -> 1; matrix products, arithmetic and copies ran while one was open for 10% -> 10% of each run, Pallas kernels for 3% -> 2%
where the time goes in v4:
time: 154 us
  Pallas kernels  127 us (82%)
  other arithmetic  13.5 us (9%)
  waiting for transfers between devices  5.3 us (3%)
  local copies, waits for them, and re-layouts  3.75 us (2%)
  between operations  1.72 us (1%)
    pallas_call x1, Pallas kernels, trade(): pl.pallas_call(functools.partial(trade_kernel, devices, early, late, cuts...  98.1 us
    pallas_call x1, Pallas kernels, gather_rows(): pl.pallas_call(functools.partial(everyone_kernel, devices), out_shape=[ta...  13.2 us
    pallas_call x1, Pallas kernels, tiles(): pl.pallas_call(tile_kernel, out_shape=jax.ShapeDtypeStruct((RB_DEV * rows...  12.4 us
    ppermute x1, waiting for transfers between devices, shards(): far = lax.ppermute(lead, 'dev', across)  5.3 us
    pallas_call x1, Pallas kernels, pack(): pl.pallas_call(functools.partial(pack_kernel, len(lanes)), out_shape=[jax...  3.6 us
  transfers between devices with their start and end apart: 1, of which 1 were waited for; matrix products, arithmetic and copies ran while one was open for 10% of the time, Pallas kernels for 2%

profile of v4, /device:TPU:0, one launch (start us, length us, event | category | flops | bytes accessed | tf_op | source)
XLA Modules:
  0.0 153.5 jit_solution(16672165992830840618)
XLA Ops:
  0.1 0.7 pad_bitcast_fusion
  0.8 1.2 pad_add_fusion.2.row_ref
  2.0 13.2 %gather_rows.1 = (s32[32,128]{1,0:T(8,128)}, s32[32,128]{1,0:T(8,128)}, bf16[64,128,128]{2,1,0:T(8,128)(2,1)}, bf16[16,128,128]{2,1,0:T(8,128)(2,1)}) custom-call(s32[2,128]{1,0:T(2,128)} %pad_add_fusion.2.row_ref, bf16[64,128,128]{2,1,0:T(8,128)(2,1)} %refs_0_.3), custom_call_target="tpu_custom_call" | custom-call | tf_op jit(solution)/shard_map/gather_rows/pallas_call | solution.py:420
  15.2 0.6 collective-permute-start.3
  15.9 1.7 %convert_reduce_fusion.1 = s32[32,64]{1,0:T(8,128)S(1)} fusion(s32[32,64]{1,0:T(8,128)} %bitcast.89, pred[64,64]{1,0:T(8,128)(4,1)S(1)} %iota_compare_fusion.10), kind=kLoop, calls=%fused_computation.144 | loop fusion | flops 522240 | bytes 20480 | tf_op jit(solution)/shard_map/reduce_sum | solution.py:33
  17.6 0.7 multiply_add_fusion
  18.3 0.1 add_add_fusion.2
  18.4 0.7 select_reduce_fusion.12
  19.1 0.1 copy.24
  19.2 0.1 copy.25
  19.4 0.8 copy.22
  20.2 0.1 copy.23
  20.3 2.9 %select_reduce_fusion.7 = s32[4,32,32]{2,1,0:T(8,128)S(1)} fusion(s32[32,128]{1,0:T(8,128)S(1)} %copy.26, s32[4,32,32]{2,1,0:T(8,128)S(1)} %copy.23), kind=kLoop, calls=%fused_computation.131 | loop fusion | flops 1568768 | bytes 49152 | tf_op jit(solution)/shard_map/reduce_sum | solution.py:41
  23.2 0.1 reshape.674
  23.6 0.1 eq.519
  23.7 0.1 eq.524
  23.8 0.1 eq.530
  23.9 0.9 select_reduce_fusion.11
  25.0 0.1 compare_reduce_fusion.3
  25.1 0.2 convert_reduce_fusion.5
  25.2 0.2 fusion.50
  25.5 0.1 fusion.53
  25.6 0.1 slice_select_fusion.1
  25.7 0.7 fusion.51
  26.4 0.1 add_bitcast_fusion
  26.5 0.7 compare_reduce_fusion.2
  27.2 0.1 convert_reduce_fusion.4
  27.4 0.3 select_reduce_fusion.14
  27.7 0.3 select_reduce_fusion.13
  28.1 0.7 select_reduce_fusion.15.send_ref
  28.8 0.1 fusion.93
  28.8 0.1 select_bitcast_fusion
  29.0 0.7 fusion.71
  29.7 0.1 constant_dynamic-slice_fusion.1
  29.7 0.1 reshape.672
  29.8 0.1 copy.27
  29.9 0.1 reshape.670
  30.0 0.1 copy.28
  30.1 0.1 reshape.671
  30.1 3.6 %pack.3.refs_4_ = bf16[37,128,128]{2,1,0:T(8,128)(2,1)} custom-call(s32[37]{0:T(128)} %select_reduce_fusion.15.send_ref, bf16[64,128,128]{2,1,0:T(8,128)(2,1)S(1)} %copy-done, bf16[64,128,128]{2,1,0:T(8,128)(2,1)} %get-tuple-element.162.refs_1_.refs_2_), custom_call_target="tpu_custom_call" | custom-call | tf_op jit(solution)/shard_map/pack/pallas_call | solution.py:333
  34.9 0.7 pad_add_fusion.3.refs_0_
  35.6 0.3 select_reduce_fusion.6
  35.9 0.6 compare_select_fusion.11.pick_ref
  36.5 5.3 %collective-permute-done.3.refs_3_.refs_2_ = bf16[16,128,128]{2,1,0:T(8,128)(2,1)S(1)} collective-permute-done((bf16[16,128,128]{2,1,0:T(8,128)(2,1)}, bf16[16,128,128]{2,1,0:T(8,128)(2,1)S(1)}, u32[]{:S(2)}, u32[]{:S(2)}) %collective-permute-start.3) | collective-permute-done | bytes 524320 | tf_op jit(solution)/shard_map/ppermute | solution.py:719
  41.8 0.8 copy-done.1
  42.6 98.1 %trade.1 = (bf16[160,128,128]{2,1,0:T(8,128)(2,1)}, bf16[192,128,128]{2,1,0:T(8,128)(2,1)}, bf16[16,128,128]{2,1,0:T(8,128)(2,1)}, bf16[37,128,128]{2,1,0:T(8,128)(2,1)}, bf16[37,128,128]{2,1,0:T(8,128)(2,1)}) custom-call(s32[176]{0:T(256)} %pad_add_fusion.3.refs_0_, bf16[64,128,128]{2,1,0:T(8,128)(2,1)S(1)} %copy-done, ...), custom_call_target="tpu_custom_call" | custom-call | tf_op jit(solution)/shard_map/trade/pallas_call | solution.py:680
  140.8 12.4 %tiles.6 = f32[2048,512]{1,0:T(8,128)} custom-call(s32[256]{0:T(256)} %compare_select_fusion.11.pick_ref, s32[64]{0:T(128)S(1)} %copy-done.2, bf16[64,128,128]{2,1,0:T(8,128)(2,1)S(1)} %copy-done, bf16[64,128,128]{2,1,0:T(8,128)(2,1)} %get-tuple-element.162.refs_1_.refs_2_, bf16[16,128,128]{2,1,0:T(8,128)(2,1)} %copy-done.1, ...), custom_call_target="tpu_custom_call" | custom-call | tf_op jit(solution)/shard_map/tiles/pallas_call | solution.py:350
  153.2 0.2 while.15
  (63 shorter events, 0.6 us)
Async XLA Ops:
  0.0 23.9 %copy-start.8 = (s32[256]{0:T(256)S(1)}, s32[256]{0:T(256)}, u32[]{:S(2)}) copy-start(s32[256]{0:T(256)} %constant.623.clone) | copy-start | bytes 3076
  0.0 23.9 %copy-start.3 = (s32[256]{0:T(256)S(1)}, s32[256]{0:T(256)}, u32[]{:S(2)}) copy-start(s32[256]{0:T(256)} %constant.624.clone) | copy-start | bytes 3076
  0.0 23.9 %copy-start.4 = (s32[256]{0:T(256)S(1)}, s32[256]{0:T(256)}, u32[]{:S(2)}) copy-start(s32[256]{0:T(256)} %constant.625.clone) | copy-start | bytes 3076
  0.0 23.9 %copy-start.9 = (s32[256]{0:T(256)S(1)}, s32[256]{0:T(256)}, u32[]{:S(2)}) copy-start(s32[256]{0:T(256)} %constant.630) | copy-start | bytes 3076
  0.0 24.9 %copy-start.10 = (pred[256]{0:T(512)(128)(4,1)S(1)}, pred[256]{0:T(512)(128)(4,1)}, u32[]{:S(2)}) copy-start(pred[256]{0:T(512)(128)(4,1)} %constant.631) | copy-start | bytes 772
  0.0 24.9 %copy-start.6 = (pred[256]{0:T(512)(128)(4,1)S(1)}, pred[256]{0:T(512)(128)(4,1)}, u32[]{:S(2)}) copy-start(pred[256]{0:T(512)(128)(4,1)} %constant.632) | copy-start | bytes 772
  0.0 24.9 %copy-start.11 = (pred[256]{0:T(512)(128)(4,1)S(1)}, pred[256]{0:T(512)(128)(4,1)}, u32[]{:S(2)}) copy-start(pred[256]{0:T(512)(128)(4,1)} %constant.633) | copy-start | bytes 772
  0.0 25.0 %copy-start.5 = (pred[256]{0:T(512)(128)(4,1)S(1)}, pred[256]{0:T(512)(128)(4,1)}, u32[]{:S(2)}) copy-start(pred[256]{0:T(512)(128)(4,1)} %constant.635) | copy-start | bytes 772
  2.0 25.4 %copy-start.7 = (s32[256]{0:T(256)S(1)}, s32[256]{0:T(256)}, u32[]{:S(2)}) copy-start(s32[256]{0:T(256)} %constant.637) | copy-start | bytes 3076
  2.0 25.4 %copy-start.12 = (pred[256]{0:T(512)(128)(4,1)S(1)}, pred[256]{0:T(512)(128)(4,1)}, u32[]{:S(2)}) copy-start(pred[256]{0:T(512)(128)(4,1)} %constant.634) | copy-start | bytes 772
  2.0 28.1 %copy-start = (bf16[64,128,128]{2,1,0:T(8,128)(2,1)S(1)}, bf16[64,128,128]{2,1,0:T(8,128)(2,1)}, u32[]{:S(2)}) copy-start(bf16[64,128,128]{2,1,0:T(8,128)(2,1)} %refs_0_.3) | copy-start | bytes 6291460
  15.2 26.6 %collective-permute-start.3 = (bf16[16,128,128]{2,1,0:T(8,128)(2,1)}, bf16[16,128,128]{2,1,0:T(8,128)(2,1)S(1)}, u32[]{:S(2)}, u32[]{:S(2)}) collective-permute-start(bf16[16,128,128]{2,1,0:T(8,128)(2,1)} %get-tuple-element.157), channel_id=1, source_target_pairs={{0,16},{1,17},{2,18},{3,19},{4,20},{5,21},{6,22},{7,23},{8,24},{9,... | collective-permute-start | bytes 1572872 | tf_op jit(solution)/shard_map/ppermute | solution.py:719
  41.8 0.8 copy-start.1
  42.6 98.1 %copy-start.2 = (s32[64]{0:T(128)S(1)}, s32[64]{0:T(128)}, u32[]{:S(2)}) copy-start(s32[64]{0:T(128)} %read_ref.1) | copy-start | bytes 772
